TPU v7x, 32 devices: a whole 2x2x4 slice. The times are simulated.
32 devices in a mesh: section: 4 (over y, x), chan: 8 (over z, core).
Axes of the slice: x: 2, y: 2, z: 4, core: 2. Of those that a mesh axis runs over, the one named last changes fastest.
Arguments:
- voltages: bfloat16 [2, 512, 524288], P(None, 'chan', 'section'), may hold values from -6 to 6
- usable: int32 [4096, 512], P(('section', 'chan')), may hold values 0 or 1
- auto_power: float32 [4096, 512], P(('section', 'chan')), may hold values from 0.5 to 4
Outputs:
- gains: float32 [2, 4096, 512], P(None, ('section', 'chan'))
Inputs may be any that keep to these rules, and one draw needn't show every extreme that they name: 1 marks a feed as usable in that channel, 0 as flagged.
All inputs are finite; a program needn't handle non-finite values. No bound on the sum of `usable` on one device may be relied on, other than what follows from the above.
Results may differ from a plain program's by a relative error of at most 0.0046.
Values may be sent and summed in bfloat16 or wider, within the bound.
A program may use at most 576 MiB of HBM per device.

v0:
```python
import math

import jax
import jax.numpy as jnp
from jax import lax
from jax.sharding import PartitionSpec as P

CHANNELS = 4096
TAPS = 4
ITERS = 5
LANES = 128


epsilon = 1e-06


def shifted_2(block, axis, distance):
    devices = range(lax.axis_size(axis))
    route = [(i - distance, i) for i in devices if i - distance in devices]
    return lax.ppermute(block, axis, route)


def prototype(tap_count, channels):
    position = lax.iota(jnp.float32, tap_count * channels)
    offset = (position - 0.5 * tap_count * channels + 0.5) / channels
    window = 0.5 - 0.5 * jnp.cos(2.0 * jnp.pi * (position + 0.5) / (tap_count * channels))
    return (jnp.sin(jnp.pi * offset) / (jnp.pi * offset) * window).reshape(tap_count, channels)


def first_table(outer):
    index = lax.iota(jnp.int32, outer)
    angles = (index[:, None] * index[None, :] % outer).astype(jnp.float32) * (2.0 * math.pi / outer)
    cosine, sine = jnp.cos(angles), jnp.sin(angles)
    return jnp.stack([jnp.stack([cosine, -sine], axis=1), jnp.stack([sine, cosine], axis=1)], axis=0)


def second_table(outer, inner, factor):
    k = lax.iota(jnp.int32, outer)[:, None, None]
    n = lax.iota(jnp.int32, inner)[None, :, None]
    j = lax.iota(jnp.int32, inner)[None, None, :]
    length = outer * inner
    angles = (n * (j * outer + k) % length).astype(jnp.float32) * (2.0 * math.pi / length)
    cosine, sine = jnp.cos(angles) * factor, jnp.sin(angles) * factor
    return jnp.stack([jnp.stack([cosine, -sine], axis=2), jnp.stack([sine, cosine], axis=2)], axis=1)


def channelize(voltages, history):
    feeds_here = voltages.shape[1]
    blocks = voltages.shape[2] // CHANNELS
    outer = CHANNELS // LANES
    extended = jnp.concatenate([history, voltages], axis=2)
    extended = extended.reshape(2, feeds_here, blocks + TAPS - 1, outer, LANES)
    extended = extended.transpose(0, 3, 2, 1, 4).astype(jnp.float32)
    coeffs = prototype(TAPS, CHANNELS).reshape(TAPS, 1, outer, 1, 1, LANES)
    filtered = coeffs[0] * extended[:, :, 0:blocks]
    for tap_index in range(1, TAPS):
        filtered = filtered + coeffs[tap_index] * extended[:, :, tap_index : tap_index + blocks]
    halfway = jnp.einsum(
        "pmbfn,pmqk->kqbfn", filtered, first_table(outer), precision=lax.Precision.HIGH
    )
    table = second_table(outer, LANES, 1.0 / math.sqrt(CHANNELS))
    spectra = jnp.einsum("kqbfn,kqnrj->krbfj", halfway, table, precision=lax.Precision.HIGH)
    return spectra.astype(jnp.bfloat16)


def local(voltages, usable, auto_power):
    outer = CHANNELS // LANES
    margin = (TAPS - 1) * CHANNELS
    tail_samples = voltages[:, :, voltages.shape[2] - margin :]
    history = shifted_2(tail_samples, "section", 1)

    small = jnp.stack([usable.astype(jnp.float32), auto_power], axis=0)
    small = lax.all_to_all(small, "chan", split_axis=2, concat_axis=1, tiled=True)
    small = lax.all_gather(small, "section", axis=1, tiled=True)
    feeds_here = small.shape[2]
    small = small.reshape(2, LANES, outer, feeds_here).transpose(0, 2, 3, 1)
    weight, power = small[0], small[1]

    spectra = channelize(voltages, history)
    blocks = spectra.shape[2]
    real = spectra[:, 0].astype(jnp.float32)
    imag = spectra[:, 1].astype(jnp.float32)
    shifted = blocks * power - jnp.sum(real * real + imag * imag, axis=1)
    now_r, now_i = weight, jnp.zeros_like(weight)
    for iteration in range(ITERS):
        ur, ui = now_r[:, None], now_i[:, None]
        proj_r = jnp.sum(real * ur + imag * ui, axis=2)
        proj_i = jnp.sum(real * ui - imag * ur, axis=2)
        rows = [proj_r, proj_i]
        if iteration > 0:
            rows.append(jnp.sum(now_r * now_r + now_i * now_i, axis=1)[:, None])
        rows = lax.psum(jnp.concatenate(rows, axis=1), "chan")
        if iteration > 0:
            inverse = 1.0 / jnp.sqrt(rows[:, 2 * blocks :] + epsilon)
            rows = rows[:, : 2 * blocks] * inverse
            now_r, now_i = now_r * inverse, now_i * inverse
        pr, pi = rows[:, :blocks, None], rows[:, blocks:, None]
        back_r = jnp.sum(real * pr - imag * pi, axis=1)
        back_i = jnp.sum(real * pi + imag * pr, axis=1)
        back_r = weight * (back_r + shifted * (weight * now_r))
        back_i = weight * (back_i + shifted * (weight * now_i))
        result = jnp.stack([back_r, back_i], axis=0)
        if iteration < ITERS - 1:
            now_r, now_i = lax.psum(result, "section")
    result = result.transpose(0, 3, 1, 2).reshape(2, CHANNELS, feeds_here)
    result = lax.psum_scatter(result, "section", scatter_dimension=1, tiled=True)
    result = lax.all_to_all(result, "chan", split_axis=1, concat_axis=2, tiled=True)
    length = jnp.sqrt(jnp.sum(result * result, axis=(0, 2)) + epsilon)
    return result / jnp.sqrt(length)[None, :, None]


def solution(mesh):
    in_specs = (
        P(None, "chan", "section"),
        P(("section", "chan"), None),
        P(("section", "chan"), None),
    )
    out_specs = P(None, ("section", "chan"), None)
    return jax.shard_map(local, mesh=mesh, in_specs=in_specs, out_specs=out_specs, check_vma=False)
```

profile of v0, /device:TPU:0, one launch (start us, length us, event | category | flops | bytes accessed | tf_op | source)
XLA Modules:
  0.0 1319.0 jit_solution(3367526858844399999)
XLA Ops:
  6.5 3.8 slice.103
  10.3 6.6 collective-permute-start
  20.4 4.9 all-to-all-start
  26.0 8.4 fusion.81
  34.4 4.4 maximum_bitcast_fusion.2
  38.7 1.8 all-to-all-done
  41.7 58.0 %collective-permute-done = bf16[2,64,12288]{2,1,0:T(8,128)(2,1)} collective-permute-done((bf16[2,64,12288]{2,1,0:T(8,128)(2,1)}, bf16[2,64,12288]{2,1,0:T(8,128)(2,1)}, u32[]{:S(2)}, u32[]{:S(2)}) %collective-permute-start) | collective-permute-done | bytes 3145760 | tf_op jit(solution)/shard_map/ppermute | solution.py:20
  99.7 35.9 %maximum_convert_fusion = f32[2,64,143360]{2,1,0:T(8,128)} fusion(bf16[2,64,131072]{2,1,0:T(8,128)(2,1)} %param.3, bf16[2,64,12288]{2,1,0:T(8,128)(2,1)} %collective-permute-done), kind=kLoop, calls=%fused_computation.55 | loop fusion | flops 73400320 | bytes 110100480 | tf_op jit(solution)/shard_map/convert_element_type | solution.py:53
  135.7 48.6 %copy.67 = f32[16,8,1120,128]{3,2,1,0:T(8,128)} copy(f32[16,8,1120,128]{3,1,2,0:T(8,128)} %bitcast.80) | data formatting | bytes 146800640
  184.3 47.7 %copy.76 = f32[2,64,35,32,128]{4,3,0,1,2:T(8,128)} copy(f32[2,64,35,32,128]{4,3,2,1,0:T(8,128)} %bitcast.82) | data formatting | bytes 146800640 | tf_op jit(solution)/shard_map/convert_element_type | solution.py:53
  232.0 112.2 %fusion.57 = f32[32,2,32,64,128,1]{4,0,3,2,1,5:T(8,128)} fusion(f32[2,32,35,64,128]{4,1,0,3,2:T(8,128)} %bitcast.269, f32[32,128]{1,0:T(8,128)S(1)} %get-tuple-element.57, f32[32,128]{1,0:T(8,128)S(1)} %get-tuple-element.58, f32[32,128]{1,0:T(8,128)S(1)} %get-tuple-element.59, f32[32,128]{1,0:T(8,128)S(1)} %get-tuple-element.56, ...), kind=kOutput, calls=%fused_computation.103 | convolution fusion | flops 6559895552 | bytes 335626240 | tf_op jit(solution)/shard_map/pmbfn,pmqk->kqbfn/dot_general | solution.py:58
  344.3 65.4 %fusion.10 = bf16[32,2,32,64,128]{4,3,2,1,0:T(8,128)(2,1)} fusion(f32[32,2,32,64,128,1]{4,0,3,2,1,5:T(8,128)} %fusion.57, f32[32,1,128,2,128]{4,2,1,3,0:T(8,128)} %get-tuple-element.45, f32[32,1,128,2,128]{4,2,1,3,0:T(8,128)} %get-tuple-element.44), kind=kOutput, calls=%fused_computation.56 | convolution fusion | flops 25788678144 | bytes 109051904 | tf_op jit(solution)/shard_map/kqbfn,kqnrj->krbfj/dot_general | solution.py:62
  409.7 3.9 copy.32
  413.6 3.8 copy.33
  417.4 21.4 %fusion.12 = (f32[32,32,128]{2,1,0:T(8,128)S(1)}, f32[32,32,128]{2,1,0:T(8,128)S(1)}) fusion(f32[32,64,128]{2,1,0:T(8,128)S(1)} %slice_bitcast_fusion.10, bf16[32,2,32,64,128]{4,3,2,1,0:T(8,128)(2,1)} %fusion.10), kind=kLoop, calls=%fused_computation.58 | loop fusion | flops 83623936 | bytes 35651584 | tf_op jit(solution)/shard_map/reduce_sum | solution.py:87
  440.5 61.3 %all-reduce.10.cloned.1.call-done = f32[32,64,128]{2,1,0:T(8,128)} async-done(((f32[32,64,128]{2,1,0:T(8,128)}), f32[32,64,128]{2,1,0:T(8,128)}) %all-reduce.10.cloned.1.call-update) | async-done | bytes 1048592 | tf_op jit(solution)/shard_map/psum | solution.py:92
  503.0 18.9 %fusion.16 = (f32[32,64,128]{2,1,0:T(8,128)S(1)}, f32[32,64,128]{2,1,0:T(8,128)S(1)}, f32[32,64,128]{2,1,0:T(8,128)S(1)}) fusion(f32[32,32,128]{2,1,0:T(8,128)S(1)} %get-tuple-element.55, f32[32,32,128]{2,1,0:T(8,128)S(1)} %get-tuple-element.54, bf16[32,2,32,64,128]{4,3,2,1,0:T(8,128)(2,1)} %fusion.10), kind=kLoop, calls=%fused_computation.62 | loop fusion | flops 116654080 | bytes 37748736 | tf_op jit(solution)/shard_map/reduce_sum | solution.py:98
  522.7 1.6 pad_maximum_fusion
  524.3 68.7 %all-reduce.12.cloned.1.call-done = f32[2,32,64,128]{3,2,1,0:T(8,128)} async-done(((f32[2,32,64,128]{3,2,1,0:T(8,128)}), f32[2,32,64,128]{3,2,1,0:T(8,128)}) %all-reduce.12.cloned.1.call-update) | async-done | bytes 2097168 | tf_op jit(solution)/shard_map/psum | solution.py:104
  593.0 1.8 add_reduce_fusion.3
  594.9 1.8 slice_bitcast_fusion.9
  596.7 21.2 %fusion.22 = (f32[32,32,128]{2,1,0:T(8,128)S(1)}, f32[32,32,128]{2,1,0:T(8,128)S(1)}) fusion(f32[32,64,128]{2,1,0:T(8,128)S(1)} %get-tuple-element.43, f32[32,64,128]{2,1,0:T(8,128)S(1)} %get-tuple-element.42, bf16[32,2,32,64,128]{4,3,2,1,0:T(8,128)(2,1)} %fusion.10), kind=kLoop, calls=%fused_computation.68 | loop fusion | flops 83623936 | bytes 36700160 | tf_op jit(solution)/shard_map/reduce_sum | solution.py:87
  619.2 60.0 %all-reduce.14.cloned.1.call-done = f32[32,65,128]{2,1,0:T(8,128)} async-done(((f32[32,65,128]{2,1,0:T(8,128)}), f32[32,65,128]{2,1,0:T(8,128)}) %all-reduce.14.cloned.1.call-update) | async-done | bytes 1064976 | tf_op jit(solution)/shard_map/psum | solution.py:92
  681.7 16.5 %fusion.26 = (f32[32,64,128]{2,1,0:T(8,128)S(1)}, f32[32,64,128]{2,1,0:T(8,128)S(1)}) fusion(f32[32,32,128]{2,1,0:T(8,128)S(1)} %get-tuple-element.53, f32[32,32,128]{2,1,0:T(8,128)S(1)} %get-tuple-element.52, bf16[32,2,32,64,128]{4,3,2,1,0:T(8,128)(2,1)} %fusion.10), kind=kLoop, calls=%fused_computation.72 | loop fusion | flops 83361792 | bytes 36700160 | tf_op jit(solution)/shard_map/reduce_sum | solution.py:98
  698.9 1.5 pad_maximum_fusion.1
  700.7 68.4 %all-reduce.16.cloned.1.call-done = f32[2,32,64,128]{3,2,1,0:T(8,128)} async-done(((f32[2,32,64,128]{3,2,1,0:T(8,128)}), f32[2,32,64,128]{3,2,1,0:T(8,128)}) %all-reduce.16.cloned.1.call-update) | async-done | bytes 2097168 | tf_op jit(solution)/shard_map/psum | solution.py:104
  769.1 1.8 add_reduce_fusion.2
  771.1 1.8 slice_bitcast_fusion.7
  772.9 21.2 %fusion.30 = (f32[32,32,128]{2,1,0:T(8,128)S(1)}, f32[32,32,128]{2,1,0:T(8,128)S(1)}) fusion(f32[32,64,128]{2,1,0:T(8,128)S(1)} %get-tuple-element.41, f32[32,64,128]{2,1,0:T(8,128)S(1)} %get-tuple-element.40, bf16[32,2,32,64,128]{4,3,2,1,0:T(8,128)(2,1)} %fusion.10), kind=kLoop, calls=%fused_computation.76 | loop fusion | flops 83623936 | bytes 36700160 | tf_op jit(solution)/shard_map/reduce_sum | solution.py:87
  795.3 60.0 %all-reduce.18.cloned.1.call-done = f32[32,65,128]{2,1,0:T(8,128)} async-done(((f32[32,65,128]{2,1,0:T(8,128)}), f32[32,65,128]{2,1,0:T(8,128)}) %all-reduce.18.cloned.1.call-update) | async-done | bytes 1064976 | tf_op jit(solution)/shard_map/psum | solution.py:92
  857.8 16.5 %fusion.34 = (f32[32,64,128]{2,1,0:T(8,128)S(1)}, f32[32,64,128]{2,1,0:T(8,128)S(1)}) fusion(f32[32,32,128]{2,1,0:T(8,128)S(1)} %get-tuple-element.51, f32[32,32,128]{2,1,0:T(8,128)S(1)} %get-tuple-element.50, bf16[32,2,32,64,128]{4,3,2,1,0:T(8,128)(2,1)} %fusion.10), kind=kLoop, calls=%fused_computation.80 | loop fusion | flops 83361792 | bytes 36700160 | tf_op jit(solution)/shard_map/reduce_sum | solution.py:98
  876.7 68.6 %all-reduce.20.cloned.1.call-done = f32[2,32,64,128]{3,2,1,0:T(8,128)} async-done(((f32[2,32,64,128]{3,2,1,0:T(8,128)}), f32[2,32,64,128]{3,2,1,0:T(8,128)}) %all-reduce.20.cloned.1.call-update) | async-done | bytes 2097168 | tf_op jit(solution)/shard_map/psum | solution.py:104
  945.3 1.8 add_reduce_fusion.1
  947.2 1.8 slice_bitcast_fusion.5
  949.0 21.2 %fusion.38 = (f32[32,32,128]{2,1,0:T(8,128)S(1)}, f32[32,32,128]{2,1,0:T(8,128)S(1)}) fusion(f32[32,64,128]{2,1,0:T(8,128)S(1)} %get-tuple-element.39, f32[32,64,128]{2,1,0:T(8,128)S(1)} %get-tuple-element.38, bf16[32,2,32,64,128]{4,3,2,1,0:T(8,128)(2,1)} %fusion.10), kind=kLoop, calls=%fused_computation.84 | loop fusion | flops 83623936 | bytes 36700160 | tf_op jit(solution)/shard_map/reduce_sum | solution.py:87
  971.5 60.0 %all-reduce.22.cloned.1.call-done = f32[32,65,128]{2,1,0:T(8,128)} async-done(((f32[32,65,128]{2,1,0:T(8,128)}), f32[32,65,128]{2,1,0:T(8,128)}) %all-reduce.22.cloned.1.call-update) | async-done | bytes 1064976 | tf_op jit(solution)/shard_map/psum | solution.py:92
  1034.0 16.5 %fusion.42 = (f32[32,64,128]{2,1,0:T(8,128)S(1)}, f32[32,64,128]{2,1,0:T(8,128)S(1)}) fusion(f32[32,32,128]{2,1,0:T(8,128)S(1)} %get-tuple-element.49, f32[32,32,128]{2,1,0:T(8,128)S(1)} %get-tuple-element.48, bf16[32,2,32,64,128]{4,3,2,1,0:T(8,128)(2,1)} %fusion.10), kind=kLoop, calls=%fused_computation.88 | loop fusion | flops 83361792 | bytes 36700160 | tf_op jit(solution)/shard_map/reduce_sum | solution.py:98
  1053.0 68.4 %all-reduce.24.cloned.1.call-done = f32[2,32,64,128]{3,2,1,0:T(8,128)} async-done(((f32[2,32,64,128]{3,2,1,0:T(8,128)}), f32[2,32,64,128]{3,2,1,0:T(8,128)}) %all-reduce.24.cloned.1.call-update) | async-done | bytes 2097168 | tf_op jit(solution)/shard_map/psum | solution.py:104
  1121.4 1.8 add_reduce_fusion
  1123.4 1.8 slice_bitcast_fusion.3
  1125.2 21.2 %fusion.46 = (f32[32,32,128]{2,1,0:T(8,128)S(1)}, f32[32,32,128]{2,1,0:T(8,128)S(1)}) fusion(f32[32,64,128]{2,1,0:T(8,128)S(1)} %get-tuple-element.37, f32[32,64,128]{2,1,0:T(8,128)S(1)} %get-tuple-element.36, bf16[32,2,32,64,128]{4,3,2,1,0:T(8,128)(2,1)} %fusion.10), kind=kLoop, calls=%fused_computation.92 | loop fusion | flops 83623936 | bytes 36700160 | tf_op jit(solution)/shard_map/reduce_sum | solution.py:87
  1147.6 60.0 %all-reduce.26.cloned.1.call-done = f32[32,65,128]{2,1,0:T(8,128)} async-done(((f32[32,65,128]{2,1,0:T(8,128)}), f32[32,65,128]{2,1,0:T(8,128)}) %all-reduce.26.cloned.1.call-update) | async-done | bytes 1064976 | tf_op jit(solution)/shard_map/psum | solution.py:92
  1210.2 16.5 %fusion.50 = (f32[32,64,128]{2,1,0:T(8,128)S(1)}, f32[32,64,128]{2,1,0:T(8,128)S(1)}) fusion(f32[32,32,128]{2,1,0:T(8,128)S(1)} %get-tuple-element.47, f32[32,32,128]{2,1,0:T(8,128)S(1)} %get-tuple-element.46, bf16[32,2,32,64,128]{4,3,2,1,0:T(8,128)(2,1)} %fusion.10), kind=kLoop, calls=%fused_computation.96 | loop fusion | flops 83361792 | bytes 36700160 | tf_op jit(solution)/shard_map/reduce_sum | solution.py:98
  1227.5 4.4 copy.47
  1232.0 51.8 %reduce-scatter.2.cloned.1.call-done = f32[2,1024,64]{2,1,0:T(8,128)} async-done(((f32[2,4096,64]{2,1,0:T(8,128)}), f32[2,1024,64]{2,1,0:T(8,128)}) %reduce-scatter.2.cloned.1.call-update) | async-done | bytes 524304 | tf_op jit(solution)/shard_map/reduce_scatter | solution.py:106
  1283.8 2.0 copy.78
  1286.9 20.0 %all_to_all.36 = f32[8,1,16384]{2,1,0:T(1,128)S(1)} all-to-all(f32[8,1,16384]{2,1,0:T(1,128)S(1)} %reshape.301), channel_id=1, replica_groups=mesh['section'=4,'chan'=8] {'chan'}, dimensions={0} | all-to-all | bytes 1048576 | tf_op jit(solution)/shard_map/all_to_all | solution.py:107
  1307.5 1.9 reduce.1
  (89 shorter events, 35.7 us)
Async XLA Ops:
  10.3 89.4 %collective-permute-start = (bf16[2,64,12288]{2,1,0:T(8,128)(2,1)}, bf16[2,64,12288]{2,1,0:T(8,128)(2,1)}, u32[]{:S(2)}, u32[]{:S(2)}) collective-permute-start(bf16[2,64,12288]{2,1,0:T(8,128)(2,1)} %slice.103), channel_id=1, source_target_pairs={{0,8},{8,16},{16,24},{1,9},{9,17},{17,25},{2,10},{10,18},{18,26},{... | collective-permute-start | bytes 9437192 | tf_op jit(solution)/shard_map/ppermute | solution.py:20
  20.4 20.2 %all-to-all-start = ((f32[2,128,512]{1,0,2:T(2,128)}), f32[2,128,512]{1,0,2:T(2,128)S(1)}, u32[]{:S(2)}, u32[]{:S(2)}) async-start(f32[2,128,512]{1,0,2:T(2,128)} %pad_maximum_fusion.9), calls=%async_computation | async-start | bytes 1048576 | tf_op jit(solution)/shard_map/all_to_all | solution.py:73
  25.2 384.4 %all-gather.2.cloned.1.call-start = ((), (), s32[]{:S(2)}) async-start(), calls=%async_computation.3 | async-start | bytes 2621440 | tf_op jit(solution)/shard_map/all_gather | solution.py:74
  41.5 460.2 %all-reduce.10.cloned.1.call-start = ((), (), s32[]{:S(2)}) async-start(), calls=%async_computation.4 | async-start | bytes 2097152 | tf_op jit(solution)/shard_map/psum | solution.py:92
  440.0 153.0 %all-reduce.12.cloned.1.call-start = ((), (), s32[]{:S(2)}) async-start(), calls=%async_computation.5 | async-start | bytes 4194304 | tf_op jit(solution)/shard_map/psum | solution.py:104
  524.3 154.9 %all-reduce.14.cloned.1.call-start = ((), (), s32[]{:S(2)}) async-start(), calls=%async_computation.6 | async-start | bytes 2359296 | tf_op jit(solution)/shard_map/psum | solution.py:92
  619.1 150.0 %all-reduce.16.cloned.1.call-start = ((), (), s32[]{:S(2)}) async-start(), calls=%async_computation.7 | async-start | bytes 4194304 | tf_op jit(solution)/shard_map/psum | solution.py:104
  679.1 19.0 %copy-start.1 = (f32[2,32,64,128]{3,2,1,0:T(8,128)S(1)}, f32[2,32,64,128]{3,2,1,0:T(8,128)}, u32[]{:S(2)}) copy-start(f32[2,32,64,128]{3,2,1,0:T(8,128)} %all-reduce.12.cloned.1.call-done) | copy-start | bytes 6291460
  700.5 154.8 %all-reduce.18.cloned.1.call-start = ((), (), s32[]{:S(2)}) async-start(), calls=%async_computation.8 | async-start | bytes 2359296 | tf_op jit(solution)/shard_map/psum | solution.py:92
  795.3 150.0 %all-reduce.20.cloned.1.call-start = ((), (), s32[]{:S(2)}) async-start(), calls=%async_computation.9 | async-start | bytes 4194304 | tf_op jit(solution)/shard_map/psum | solution.py:104
  855.3 19.0 %copy-start.2 = (f32[2,32,64,128]{3,2,1,0:T(8,128)S(1)}, f32[2,32,64,128]{3,2,1,0:T(8,128)}, u32[]{:S(2)}) copy-start(f32[2,32,64,128]{3,2,1,0:T(8,128)} %all-reduce.16.cloned.1.call-done) | copy-start | bytes 6291460
  876.6 154.8 %all-reduce.22.cloned.1.call-start = ((), (), s32[]{:S(2)}) async-start(), calls=%async_computation.10 | async-start | bytes 2359296 | tf_op jit(solution)/shard_map/psum | solution.py:92
  971.4 150.0 %all-reduce.24.cloned.1.call-start = ((), (), s32[]{:S(2)}) async-start(), calls=%async_computation.11 | async-start | bytes 4194304 | tf_op jit(solution)/shard_map/psum | solution.py:104
  1031.4 19.0 %copy-start.3 = (f32[2,32,64,128]{3,2,1,0:T(8,128)S(1)}, f32[2,32,64,128]{3,2,1,0:T(8,128)}, u32[]{:S(2)}) copy-start(f32[2,32,64,128]{3,2,1,0:T(8,128)} %all-reduce.20.cloned.1.call-done) | copy-start | bytes 6291460
  1052.8 154.8 %all-reduce.26.cloned.1.call-start = ((), (), s32[]{:S(2)}) async-start(), calls=%async_computation.12 | async-start | bytes 2359296 | tf_op jit(solution)/shard_map/psum | solution.py:92
  1147.6 136.2 %reduce-scatter.2.cloned.1.call-start = ((), (), s32[]{:S(2)}) async-start(), calls=%async_computation.13 | async-start | bytes 5242880 | tf_op jit(solution)/shard_map/reduce_scatter | solution.py:106
  1207.6 19.0 %copy-start = (f32[2,32,64,128]{3,2,1,0:T(8,128)S(1)}, f32[2,32,64,128]{3,2,1,0:T(8,128)}, u32[]{:S(2)}) copy-start(f32[2,32,64,128]{3,2,1,0:T(8,128)} %all-reduce.24.cloned.1.call-done) | copy-start | bytes 6291460
Sparse Core Ops, SparseCore 0:
  41.6 49.6 all-gather.1
  440.1 61.5 all-reduce.9
  524.4 68.5 all-reduce.11
  619.3 59.8 all-reduce.13
  700.6 68.5 all-reduce.15
  795.4 59.8 all-reduce.17
  876.7 68.5 all-reduce.19
  971.6 59.8 all-reduce.21
  1052.9 68.5 all-reduce.23
  1147.7 59.8 all-reduce.25
  1232.1 51.6 reduce-scatter.1
where the time goes:
time: 1330 us; the launch traced here: 1320 us
  waiting for transfers between devices  687 us (52%)
  other arithmetic  276 us (21%)
  matrix products  178 us (13%)
  local copies, waits for them, and re-layouts  131 us (10%)
  blocking collectives  20 us (2%)
  between operations  14 us (1%)
    psum x5, waiting for transfers between devices, local(): rows = lax.psum(jnp.concatenate(rows, axis=1), 'chan')  301 us
    psum x4, waiting for transfers between devices, local(): now_r, now_i = lax.psum(result, 'section')  274 us
    dot_general x1, matrix products, channelize(): jnp.einsum('pmbfn,pmqk->kqbfn', filtered, first_table(outer), precision=l...  112 us
    reduce_sum x5, other arithmetic, local(): proj_r = jnp.sum(real * ur + imag * ui, axis=2)  106 us
    reduce_sum x5, other arithmetic, local(): back_r = jnp.sum(real * pr - imag * pi, axis=1)  84.8 us
    dot_general x1, matrix products, channelize(): jnp.einsum('kqbfn,kqnrj->krbfj', halfway, table, precision=lax.Precision....  65.4 us
    ppermute x1, waiting for transfers between devices, shifted_2(): return lax.ppermute(block, axis, route)  58 us
    unnamed x17, local copies, waits for them, and re-layouts  53 us
  transfers between devices with their start and end apart: 13, of which 12 were waited for; matrix products, arithmetic and copies ran while one was open for 25% of the time, Pallas kernels for 0%

commit v1 on v0

v1 whole, which is shorter than its diff:
```python
import functools
import math

import jax
import jax.numpy as jnp
import numpy as np
from jax import lax
from jax.experimental import pallas as pl
from jax.experimental.pallas import tpu as pltpu
from jax.sharding import PartitionSpec as P

CHANNELS = 4096
TAPS = 4
ITERS = 5
LANES = 128
OUTER = CHANNELS // LANES
TILE = 16
epsilon = 1e-06
F32 = jnp.float32
BF16 = jnp.bfloat16
VMEM_LIMIT = 60 * 1024 * 1024


def prototype():
    position = np.arange(TAPS * CHANNELS, dtype=np.float64)
    offset = (position - 0.5 * TAPS * CHANNELS + 0.5) / CHANNELS
    window = 0.5 - 0.5 * np.cos(2.0 * np.pi * (position + 0.5) / (TAPS * CHANNELS))
    taps = np.sin(np.pi * offset) / (np.pi * offset) * window
    return taps.astype(np.float32).reshape(TAPS, OUTER, LANES)


def second_table():
    j = np.arange(LANES)
    twist = np.exp(-2j * np.pi * (np.outer(np.arange(OUTER), j) % CHANNELS) / CHANNELS)
    inner = np.exp(-2j * np.pi * (np.outer(j, j) % LANES) / LANES) / math.sqrt(CHANNELS)
    tr, ti = (jnp.asarray(a.astype(np.float32))[:, :, None] for a in (twist.real, twist.imag))
    fr, fi = (jnp.asarray(a.astype(np.float32))[None] for a in (inner.real, inner.imag))
    re, im = tr * fr - ti * fi, tr * fi + ti * fr
    table = jnp.concatenate(
        [jnp.concatenate([re, im], axis=2), jnp.concatenate([-im, re], axis=2)], axis=1
    )
    high = table.astype(BF16)
    low = (table - lax.optimization_barrier(high).astype(F32)).astype(BF16)
    return high, low


def times(z, w):
    zr, zi = z
    wr, wi = float(w.real), float(w.imag)
    if abs(wi) < 1e-12 and abs(wr - 1) < 1e-12:
        return zr, zi
    if abs(wr) < 1e-12 and abs(wi + 1) < 1e-12:
        return zi, -zr
    half = math.sqrt(0.5)
    if abs(wr - half) < 1e-12 and abs(wi + half) < 1e-12:
        return (zr + zi) * half, (zi - zr) * half
    if abs(wr + half) < 1e-12 and abs(wi + half) < 1e-12:
        return (zi - zr) * half, (zr + zi) * -half
    return zr * wr - zi * wi, zr * wi + zi * wr


def plus(a, b):
    return a[0] + b[0], a[1] + b[1]


def minus(a, b):
    return a[0] - b[0], a[1] - b[1]


def dft(values):
    n = len(values)
    if n == 1:
        return values
    even, odd = dft(values[0::2]), dft(values[1::2])
    odd = [times(z, np.exp(-2j * np.pi * k / n)) for k, z in enumerate(odd)]
    return [plus(a, b) for a, b in zip(even, odd)] + [minus(a, b) for a, b in zip(even, odd)]


QUICK = 8
SLOW = OUTER // QUICK


def channelize_kernel(lead, frames, x_ref, prev_ref, taps_ref, high_ref, low_ref, *rest):
    out_ref, filtered, quick, ah, al, bh, bl = rest[-7:]
    rows = frames * TILE

    def filter_step(m, carry):
        column = m * LANES
        taps = [taps_ref[t, pl.ds(m, 1), :] for t in range(TAPS)]
        for part in range(2):
            window = []
            for frame in range(1 - TAPS, frames):
                if frame < 0:
                    at = pl.multiple_of((lead + frame) * CHANNELS + column, LANES)
                    tile = prev_ref[part, :, pl.ds(at, LANES)]
                else:
                    at = pl.multiple_of(frame * CHANNELS + column, LANES)
                    tile = x_ref[part, :, pl.ds(at, LANES)]
                window.append(tile.astype(F32))
            for b in range(frames):
                total = window[b] * taps[0]
                for t in range(1, TAPS):
                    total = total + window[b + t] * taps[t]
                filtered[m, part, b * TILE : (b + 1) * TILE, :] = total
        return carry

    lax.fori_loop(0, OUTER, filter_step, 0)

    def quick_step(r, carry):
        at = pl.ds(pl.multiple_of(r * 8, 8), 8)
        for m0 in range(SLOW):
            values = [
                tuple(filtered[m1 * SLOW + m0, part, at, :] for part in range(2))
                for m1 in range(QUICK)
            ]
            for k, z in enumerate(dft(values)):
                z = times(z, np.exp(-2j * np.pi * m0 * k / OUTER))
                for part in range(2):
                    quick[k, m0, part, at, :] = z[part]
        return carry

    lax.fori_loop(0, rows // 8, quick_step, 0)

    def slow_step(k, hi_ref, lo_ref):
        for r in range(0, rows, TILE):
            at = slice(r, r + TILE)
            values = [
                tuple(quick[k, m0, part, at, :] for part in range(2)) for m0 in range(SLOW)
            ]
            for i, z in enumerate(dft(values)):
                for part in range(2):
                    hi = z[part].astype(BF16)
                    lo = (z[part] - hi.astype(F32)).astype(BF16)
                    hi_ref[i, at, part * LANES : (part + 1) * LANES] = hi
                    lo_ref[i, at, part * LANES : (part + 1) * LANES] = lo

    def matmul_step(k, hi_ref, lo_ref):
        for i in range(SLOW):
            k1 = i * QUICK + k
            hi, lo = hi_ref[i], lo_ref[i]
            th, tl = high_ref[k1], low_ref[k1]
            dot = functools.partial(jnp.dot, preferred_element_type=F32)
            res = (dot(hi, th) + dot(lo, th)) + dot(hi, tl)
            for part in range(2):
                piece = res[:, part * LANES : (part + 1) * LANES].astype(BF16)
                out_ref[k1, part, 0] = piece.reshape(frames, TILE, LANES)

    slow_step(0, ah, al)

    def pair_step(i, carry):
        k = 2 * i
        slow_step(k + 1, bh, bl)
        matmul_step(k, ah, al)
        slow_step(jnp.minimum(k + 2, QUICK - 1), ah, al)
        matmul_step(k + 1, bh, bl)
        return carry

    lax.fori_loop(0, QUICK // 2, pair_step, 0)


def channelize(voltages, before, high, low, earlier):
    feeds_here = voltages.shape[1]
    blocks = voltages.shape[2] // CHANNELS
    frames = 8
    first = 0 if before is not None else 1
    steps = 1 if before is not None else blocks // frames - 1
    lead = TAPS - 1 if before is not None else 4
    if before is None:
        before = voltages
    per = frames // 4
    if lead == 4:
        before_map = lambda f, b: (0, f, (b + first) * per - 1)
    else:
        before_map = lambda f, b: (0, f, 0)
    in_specs = [
        pl.BlockSpec((2, TILE, frames * CHANNELS), lambda f, b: (0, f, b + first)),
        pl.BlockSpec((2, TILE, lead * CHANNELS), before_map),
        pl.BlockSpec((TAPS, OUTER, LANES), lambda f, b: (0, 0, 0)),
        pl.BlockSpec((OUTER, 2 * LANES, 2 * LANES), lambda f, b: (0, 0, 0)),
        pl.BlockSpec((OUTER, 2 * LANES, 2 * LANES), lambda f, b: (0, 0, 0)),
    ]
    args = [voltages, before, jnp.asarray(prototype()), high, low]
    aliases = {}
    if earlier is not None:
        in_specs.append(pl.BlockSpec(memory_space=pl.ANY))
        args.append(earlier)
        aliases = {5: 0}
    rows = frames * TILE
    share = steps * frames * feeds_here
    return pl.pallas_call(
        functools.partial(channelize_kernel, lead, frames),
        grid=(feeds_here // TILE, steps),
        in_specs=in_specs,
        out_specs=pl.BlockSpec(
            (OUTER, 2, 1, frames, TILE, LANES), lambda f, b: (0, 0, f, b + first, 0, 0)
        ),
        out_shape=jax.ShapeDtypeStruct(
            (OUTER, 2, feeds_here // TILE, blocks, TILE, LANES), BF16
        ),
        scratch_shapes=[
            pltpu.VMEM((OUTER, 2, rows, LANES), F32),
            pltpu.VMEM((QUICK, SLOW, 2, rows, LANES), F32),
        ]
        + [pltpu.VMEM((SLOW, rows, 2 * LANES), BF16)] * 4,
        input_output_aliases=aliases,
        compiler_params=pltpu.CompilerParams(
            dimension_semantics=("arbitrary", "arbitrary"), vmem_limit_bytes=VMEM_LIMIT
        ),
        cost_estimate=pl.CostEstimate(
            flops=share * CHANNELS * 2 * 256 * 6,
            bytes_accessed=share * CHANNELS * 8,
            transcendentals=0,
        ),
    )(*args)


def fold_rows(parts):
    row = lax.broadcasted_iota(jnp.int32, (8, LANES), 0)
    half = []
    for i in range(4):
        a, b = parts[i], parts[i + 4]
        keep = jnp.where(row < 4, a, b)
        move = jnp.where(row < 4, b, a)
        half.append(keep + pltpu.roll(move, 4, 0))
    for shift in (2, 1):
        count = len(half) // 2
        bit = (row & shift) == 0
        half = [
            jnp.where(
                bit,
                half[i] + pltpu.roll(half[i], 8 - shift, 0),
                half[i + count] + pltpu.roll(half[i + count], shift, 0),
            )
            for i in range(count)
        ]
    return half[0]


def solve_kernel(sizes, *refs):
    n_section, n_chan, feeds, blocks, chunks, kc = sizes
    (spectra_hbm, weight_ref, power_ref, out_ref,
     spectra, diagonal, local_p, half_in, half_sum, piece_in, full_p, scaled,
     norm, local_q, q_in, y_ref,
     load_sem, half_ss, half_rs, piece_ss, piece_rs, gather_ss, gather_rs,
     share_ss, share_rs, norm_ss, norm_rs, q_ss, q_rs, y_ss, y_rs) = refs
    tiles = feeds // TILE
    n_z = n_chan // 2
    me_s = lax.axis_index("section")
    me_c = lax.axis_index("chan")
    core, z = me_c % 2, me_c // 2
    half_k = kc // 2
    half_rows = half_k * 2 * blocks
    piece_rows = half_rows // n_z
    k_piece = kc // n_section

    def remote(src, dst, ss, rs, **where):
        return pltpu.make_async_remote_copy(
            src_ref=src, dst_ref=dst, send_sem=ss, recv_sem=rs,
            device_id=where, device_id_type=pl.DeviceIdType.MESH,
        )

    def load(c):
        at = pl.ds(c * kc, kc)
        return pltpu.make_async_copy(spectra_hbm.at[at], spectra.at[at], load_sem.at[c])

    def half_copy(c):
        return remote(local_p.at[c, 1 - core], half_in.at[c], half_ss.at[c], half_rs.at[c],
                      chan=z * 2 + (1 - core))

    def norm_copies(c):
        return [
            remote(norm.at[c, 0], norm.at[c, d], norm_ss.at[c, d - 1], norm_rs.at[c, d - 1],
                   chan=(me_c + d) % n_chan)
            for d in range(1, n_chan)
        ]

    def piece_copies(c):
        copies = []
        for d in range(1, n_z):
            to = (z + d) % n_z
            rows = pl.ds(pl.multiple_of(to * piece_rows, piece_rows), piece_rows)
            copies.append(remote(half_sum.at[c, rows], piece_in.at[c, d - 1],
                                 piece_ss.at[c, d - 1], piece_rs.at[c, d - 1],
                                 chan=to * 2 + core))
        return copies

    def gather_copies(c, receive=False):
        copies = []
        for d in range(1, n_z):
            to = (z + d) % n_z
            owner = (z - d + n_z) % n_z if receive else z
            rows = pl.ds(pl.multiple_of(owner * piece_rows, piece_rows), piece_rows)
            view = full_p.at[c, core, rows]
            copies.append(remote(view, view, gather_ss.at[c, d - 1], gather_rs.at[c, d - 1],
                                 chan=to * 2 + core))
        return copies

    def share_copy(c, receive=False):
        view = full_p.at[c, 1 - core if receive else core]
        return remote(view, view, share_ss.at[c], share_rs.at[c], chan=z * 2 + (1 - core))

    def q_copies(c):
        copies = []
        for d in range(1, n_section):
            to = (me_s + d) % n_section
            copies.append(remote(local_q.at[c, pl.ds(to * k_piece, k_piece)], q_in.at[c, d - 1],
                                 q_ss.at[c, d - 1], q_rs.at[c, d - 1], section=to))
        return copies

    def y_copies(c, receive=False):
        copies = []
        for d in range(1, n_section):
            to = (me_s + d) % n_section
            owner = (me_s - d + n_section) % n_section if receive else me_s
            view = y_ref.at[c, pl.ds(owner * k_piece, k_piece)]
            copies.append(remote(view, view, y_ss.at[c, d - 1], y_rs.at[c, d - 1], section=to))
        return copies

    def pair(k1, tile, b):
        return spectra[k1, 0, tile, b].astype(F32), spectra[k1, 1, tile, b].astype(F32)

    def project(it, c):
        @pl.when(it == 0)
        def _():
            load(c).wait()

        @pl.when(it > 0)
        def _():
            for copy in y_copies(c):
                copy.wait_send()
            for copy in y_copies(c, receive=True):
                copy.wait_recv()

        def one(k, carry):
            k1 = c * kc + k
            yr = [y_ref[c, k, 0, t * TILE : (t + 1) * TILE, :].astype(F32) for t in range(tiles)]
            yi = [y_ref[c, k, 1, t * TILE : (t + 1) * TILE, :].astype(F32) for t in range(tiles)]
            square = sum(a * a for a in yr + yi)
            norm[c, 0, pl.ds(k, 1), :] = jnp.sum(square, axis=0, keepdims=True)

            def group(g, carry):
                rows_r, rows_i = [], []
                for s in range(8):
                    b = g * 8 + s
                    ar = ai = None
                    for t in range(tiles):
                        re, im = pair(k1, t, b)
                        pr = re * yr[t] + im * yi[t]
                        pi = re * yi[t] - im * yr[t]
                        ar = pr if ar is None else ar + pr
                        ai = pi if ai is None else ai + pi
                    rows_r.append(ar[:8] + ar[8:])
                    rows_i.append(ai[:8] + ai[8:])
                at = (k % half_k) * (2 * blocks) + g * 8
                h = k // half_k
                local_p[c, h, pl.ds(pl.multiple_of(at, 8), 8), :] = fold_rows(rows_r)
                at = at + blocks
                local_p[c, h, pl.ds(pl.multiple_of(at, 8), 8), :] = fold_rows(rows_i)
                return carry

            lax.fori_loop(0, blocks // 8, group, 0)
            return carry

        lax.fori_loop(0, kc, one, 0)
        half_copy(c).start()
        for copy in norm_copies(c):
            copy.start()

        @pl.when(it == 0)
        def _():
            def one_d(k, carry):
                k1 = c * kc + k

                def step(b, totals):
                    new = []
                    for t in range(tiles):
                        re, im = pair(k1, t, b)
                        new.append(totals[t] + (re * re + im * im))
                    return tuple(new)

                zero = jnp.zeros((TILE, LANES), F32)
                totals = lax.fori_loop(0, blocks, step, (zero,) * tiles)
                for t in range(tiles):
                    at = slice(t * TILE, (t + 1) * TILE)
                    diagonal[k1, at, :] = blocks * power_ref[k1, at, :] - totals[t]
                return carry

            lax.fori_loop(0, kc, one_d, 0)

    def add_half(it, c):
        half_copy(c).wait()
        half_sum[c] = local_p[c, core] + half_in[c]
        for copy in piece_copies(c):
            copy.start()

    def add_pieces(it, c):
        for copy in piece_copies(c):
            copy.wait()
        rows = pl.ds(pl.multiple_of(z * piece_rows, piece_rows), piece_rows)
        total = half_sum[c, rows, :]
        for d in range(1, n_z):
            total = total + piece_in[c, d - 1]
        full_p[c, core, rows, :] = total
        for copy in gather_copies(c):
            copy.start()

    def share_half(it, c):
        for copy in gather_copies(c):
            copy.wait_send()
        for copy in gather_copies(c, receive=True):
            copy.wait_recv()
        share_copy(c).start()

    def expand(it, c):
        share_copy(c).wait_send()
        share_copy(c, receive=True).wait_recv()
        for copy in norm_copies(c):
            copy.wait()
        length = norm[c, 0]
        for d in range(1, n_chan):
            length = length + norm[c, d]
        inverse = jnp.where(it == 0, 1.0, 1.0 / jnp.sqrt(length + epsilon))
        norm_scale = scaled.at[pl.ds(2 * blocks, 8)]
        norm_scale[...] = inverse

        def one(k, carry):
            k1 = c * kc + k
            inv = scaled[pl.ds(2 * blocks + k, 1), :]
            at = pl.multiple_of((k % half_k) * (2 * blocks), 2 * blocks)
            scaled[0 : 2 * blocks, :] = full_p[c, k // half_k, pl.ds(at, 2 * blocks), :] * inv

            def group(g, totals):
                totals = list(totals)
                for s in range(4):
                    b = g * 4 + s
                    pr = scaled[pl.ds(b, 1), :]
                    pi = scaled[pl.ds(blocks + b, 1), :]
                    for t in range(tiles):
                        re, im = pair(k1, t, b)
                        totals[2 * t] = totals[2 * t] + (re * pr - im * pi)
                        totals[2 * t + 1] = totals[2 * t + 1] + (re * pi + im * pr)
                return tuple(totals)

            zero = jnp.zeros((TILE, LANES), F32)
            totals = lax.fori_loop(0, blocks // 4, group, (zero,) * (2 * tiles))
            for t in range(tiles):
                at = slice(t * TILE, (t + 1) * TILE)
                weight = weight_ref[k1, at, :]
                shift = diagonal[k1, at, :] * inv
                for part in range(2):
                    now = y_ref[c, k, part, at, :].astype(F32)
                    value = weight * (totals[2 * t + part] + shift * now)
                    local_q[c, k, part, at, :] = value.astype(BF16)
            return carry

        lax.fori_loop(0, kc, one, 0)
        for copy in q_copies(c):
            copy.start()

    def add_sections(it, c):
        for copy in q_copies(c):
            copy.wait()
        for k in range(k_piece):
            for part in range(2):
                at = me_s * k_piece + k
                total = local_q[c, at, part].astype(F32)
                for d in range(1, n_section):
                    total = total + q_in[c, d - 1, k, part].astype(F32)
                y_ref[c, at, part] = total.astype(BF16)
        for copy in y_copies(c):
            copy.start()

    barrier = pltpu.get_barrier_semaphore()
    for d in range(1, n_chan):
        pl.semaphore_signal(barrier, inc=1, device_id={"chan": (me_c + d) % n_chan},
                            device_id_type=pl.DeviceIdType.MESH)
    for d in range(1, n_section):
        pl.semaphore_signal(barrier, inc=1, device_id={"section": (me_s + d) % n_section},
                            device_id_type=pl.DeviceIdType.MESH)

    @pl.loop(0, chunks)
    def _(c):
        load(c).start()

    @pl.loop(0, chunks)
    def _(c):
        for k in range(kc):
            y_ref[c, k, 0] = weight_ref[c * kc + k].astype(BF16)
            y_ref[c, k, 1] = jnp.zeros((feeds, LANES), BF16)
        norm[c, 0] = jnp.zeros((8, LANES), F32)

    pl.semaphore_wait(barrier, n_chan + n_section - 2)

    stages = [project, add_half, add_pieces, share_half, expand, add_sections]
    period = max(chunks, len(stages) + 1)

    @pl.loop(0, ITERS * period + len(stages))
    def _(slot):
        for lag, stage in reversed(list(enumerate(stages))):
            turn = slot - lag + period
            it, c = turn // period - 1, turn % period

            @pl.when((it >= 0) & (it < ITERS) & (c < chunks))
            def _():
                stage(it, c)

    @pl.loop(0, chunks)
    def _(c):
        for copy in y_copies(c):
            copy.wait_send()
        for copy in y_copies(c, receive=True):
            copy.wait_recv()

    out_ref[...] = y_ref[...]


def solve(spectra, weight, power, n_section, n_chan):
    feeds, blocks = spectra.shape[2] * TILE, spectra.shape[3]
    kc = n_section
    chunks = OUTER // kc
    n_z = n_chan // 2
    half_rows = kc * blocks
    piece_rows = half_rows // n_z
    k_piece = kc // n_section
    dma = pltpu.SemaphoreType.DMA
    per = lambda n: dma((chunks, n))
    scratch = [
        pltpu.VMEM(spectra.shape, BF16),
        pltpu.VMEM((OUTER, feeds, LANES), F32),
        pltpu.VMEM((chunks, 2, half_rows, LANES), F32),
        pltpu.VMEM((chunks, half_rows, LANES), F32),
        pltpu.VMEM((chunks, half_rows, LANES), F32),
        pltpu.VMEM((chunks, n_z - 1, piece_rows, LANES), F32),
        pltpu.VMEM((chunks, 2, half_rows, LANES), F32),
        pltpu.VMEM((2 * blocks + 8, LANES), F32),
        pltpu.VMEM((chunks, n_chan, 8, LANES), F32),
        pltpu.VMEM((chunks, kc, 2, feeds, LANES), BF16),
        pltpu.VMEM((chunks, n_section - 1, k_piece, 2, feeds, LANES), BF16),
        pltpu.VMEM((chunks, kc, 2, feeds, LANES), BF16),
        dma((chunks,)),
        dma((chunks,)), dma((chunks,)),
        per(n_z - 1), per(n_z - 1), per(n_z - 1), per(n_z - 1),
        dma((chunks,)), dma((chunks,)),
        per(n_chan - 1), per(n_chan - 1),
        per(n_section - 1), per(n_section - 1), per(n_section - 1), per(n_section - 1),
    ]
    vmem = pl.BlockSpec(memory_space=pltpu.VMEM)
    return pl.pallas_call(
        functools.partial(solve_kernel, (n_section, n_chan, feeds, blocks, chunks, kc)),
        in_specs=[pl.BlockSpec(memory_space=pl.ANY), vmem, vmem],
        out_specs=vmem,
        out_shape=jax.ShapeDtypeStruct((chunks, kc, 2, feeds, LANES), BF16),
        scratch_shapes=scratch,
        compiler_params=pltpu.CompilerParams(
            collective_id=1, has_side_effects=True, vmem_limit_bytes=VMEM_LIMIT
        ),
    )(spectra, weight, power)


def local(voltages, usable, auto_power):
    n_section, n_chan = lax.axis_size("section"), lax.axis_size("chan")
    margin = (TAPS - 1) * CHANNELS
    tail = voltages[:, :, voltages.shape[2] - margin :]
    history = lax.ppermute(tail, "section", [(i, i + 1) for i in range(n_section - 1)])

    small = jnp.stack([usable.astype(F32), auto_power], axis=0)
    small = lax.all_to_all(small, "chan", split_axis=2, concat_axis=1, tiled=True)
    small = lax.all_gather(small, "section", axis=1, tiled=True)
    feeds_here = small.shape[2]
    small = small.reshape(2, LANES, OUTER, feeds_here).transpose(0, 2, 3, 1)

    high, low = second_table()
    spectra = channelize(voltages, None, high, low, None)
    spectra = channelize(voltages, history, high, low, spectra)

    result = solve(spectra, small[0], small[1], n_section, n_chan)
    result = result.reshape(OUTER, 2, feeds_here, LANES)
    width = LANES // n_section
    result = lax.dynamic_slice_in_dim(result, lax.axis_index("section") * width, width, axis=3)
    result = result.transpose(1, 3, 0, 2).reshape(2, width * OUTER, feeds_here)
    result = lax.all_to_all(result, "chan", split_axis=1, concat_axis=2, tiled=True)
    result = result.astype(F32)
    length = jnp.sqrt(jnp.sum(result * result, axis=(0, 2)) + epsilon)
    return result / jnp.sqrt(length)[None, :, None]


def solution(mesh):
    in_specs = (
        P(None, "chan", "section"),
        P(("section", "chan"), None),
        P(("section", "chan"), None),
    )
    out_specs = P(None, ("section", "chan"), None)
    return jax.shard_map(local, mesh=mesh, in_specs=in_specs, out_specs=out_specs, check_vma=False)
```

time: 1330 us -> 429 us (0.32)
  waiting for transfers between devices: 687 us -> 3.68 us
  Pallas kernels: 0 us -> 351 us
  other arithmetic: 276 us -> 15.5 us
  matrix products: 178 us -> 0 us
  local copies, waits for them, and re-layouts: 131 us -> 21.4 us
    psum x9 -> x0, waiting for transfers between devices: 575 us -> none  [the longest x5 301 us: local(): rows = lax.psum(jnp.concatenate(rows, axis=1), 'chan')]
    pallas_call x0 -> x3, Pallas kernels: none -> 351 us  [the longest x1 253 us: solve(): pl.pallas_call(functools.partial(solve_kernel, (n_section, n_chan, feeds,...]
    reduce_sum x14 -> x0, other arithmetic: 198 us -> none  [the longest x5 106 us: local(): proj_r = jnp.sum(real * ur + imag * ui, axis=2)]
    dot_general x2 -> x0, matrix products: 178 us -> none  [the longest x1 112 us: channelize(): jnp.einsum('pmbfn,pmqk->kqbfn', filtered, first_table(outer), precision=l...]
    ppermute x1, waiting for transfers between devices: 58 us -> 0.01 us  [local(): lax.ppermute(tail, 'section', [(i, i + 1) for i in range(n_section - 1)])]
    reduce_scatter x1 -> x0, waiting for transfers between devices: 51.8 us -> none  [local(): lax.psum_scatter(result, 'section', scatter_dimension=1, tiled=True)]
    unnamed x17 -> x14, local copies, waits for them, and re-layouts: 53 us -> 3.89 us
    convert_element_type x1, local copies, waits for them, and re-layouts: 47.7 us -> 0.1 us  [local(): result = result.astype(F32)]
  transfers between devices with their start and end apart: 13 -> 3, of which waited for: 12 -> 1; matrix products, arithmetic and copies ran while one was open for 25% -> 4% of each run, Pallas kernels for 0% -> 23%
where the time goes in v1:
time: 429 us
  Pallas kernels  351 us (82%)
  local copies, waits for them, and re-layouts  21.4 us (5%)
  other arithmetic  15.5 us (4%)
  between operations  13.6 us (3%)
  blocking collectives  12.2 us (3%)
  starting transfers between devices  11.4 us (3%)
    pallas_call x1, Pallas kernels, solve(): pl.pallas_call(functools.partial(solve_kernel, (n_section, n_chan, feeds,...  253 us
    pallas_call x2, Pallas kernels, channelize(): pl.pallas_call(functools.partial(channelize_kernel, lead, frames), grid=(...  98.3 us
    all_to_all x1, blocking collectives, local(): lax.all_to_all(result, 'chan', split_axis=1, concat_axis=2, tiled=True)  12.2 us
  transfers between devices with their start and end apart: 3, of which 1 were waited for; matrix products, arithmetic and copies ran while one was open for 4% of the time, Pallas kernels for 23%

profile of v1, /device:TPU:0, one launch (start us, length us, event | category | flops | bytes accessed | tf_op | source)
XLA Modules:
  0.0 429.0 jit_solution(4527727274804142475)
XLA Ops:
  6.5 1.1 copy.42
  7.6 1.1 copy.43
  8.7 0.0 copy-start
  8.7 0.0 copy-start.1
  8.7 0.0 copy-start.2
  8.8 0.0 copy-start.3
  8.8 1.3 pad_maximum_fusion
  10.0 6.4 %all-to-all-start = ((f32[2,128,512]{1,0,2:T(2,128)}), f32[2,128,512]{1,0,2:T(2,128)S(1)}, u32[]{:S(2)}, u32[]{:S(2)}) async-start(f32[2,128,512]{1,0,2:T(2,128)} %pad_maximum_fusion), calls=%async_computation | async-start | bytes 1048576 | tf_op jit(solution)/shard_map/all_to_all | solution.py:567
  16.4 0.0 all-gather.2.cloned.1.call-start
  16.4 3.9 slice.9
  20.3 5.1 %collective-permute-start = (bf16[2,64,12288]{2,1,0:T(8,128)(2,1)}, bf16[2,64,12288]{2,1,0:T(8,128)(2,1)}, u32[]{:S(2)}, u32[]{:S(2)}) collective-permute-start(bf16[2,64,12288]{2,1,0:T(8,128)(2,1)} %slice.9), channel_id=1, source_target_pairs={{0,8},{8,16},{16,24},{1,9},{9,17},{17,25},{2,10},{10,18},{18,26},{... | collective-permute-start | bytes 9437192 | tf_op jit(solution)/shard_map/ppermute | solution.py:564
  25.4 0.0 copy-done
  25.4 0.0 copy-done.1
  25.4 0.0 copy-done.2
  25.4 0.0 copy-done.3
  25.4 2.7 multiply_add_fusion
  28.1 3.7 all-to-all-done
  31.8 0.8 copy.58
  32.6 0.0 all-gather.2.cloned.1.call-update
  32.6 5.0 %fusion.high_ref = bf16[32,256,256]{2,1,0:T(8,128)(2,1)} fusion(f32[32,128,128]{2,1,0:T(8,128)} %get-tuple-element.9, f32[32,128,128]{2,1,0:T(8,128)} %get-tuple-element.8, f32[32,128,128]{2,1,0:T(8,128)S(1)} %get-tuple-element.7), kind=kLoop, calls=%fused_computation.2 | loop fusion | flops 16777216 | bytes 10485760 | tf_op jit(solution)/shard_map/convert_element_type | solution.py:42
  37.7 6.3 %subtract_convert_fusion.low_ref = bf16[32,256,256]{2,1,0:T(8,128)(2,1)} fusion(bf16[32,256,256]{2,1,0:T(8,128)(2,1)} %fusion.high_ref, f32[32,128,128]{2,1,0:T(8,128)} %get-tuple-element.9, f32[32,128,128]{2,1,0:T(8,128)} %get-tuple-element.8, f32[32,128,128]{2,1,0:T(8,128)S(1)} %get-tuple-element.7), kind=kLoop, calls=%fused_computation.1 | loop fusion | flops 12582912 | bytes 14680064 | tf_op jit(solution)/shard_map/convert_element_type | solution.py:43
  44.0 71.1 %shard_map.91.rest_0_ = bf16[32,2,4,32,16,128]{5,4,3,2,1,0:T(8,128)(2,1)} custom-call(bf16[2,64,131072]{2,1,0:T(8,128)(2,1)} %x_ref.3, bf16[2,64,131072]{2,1,0:T(8,128)(2,1)} %x_ref.3, f32[4,32,128]{2,1,0:T(8,128)} %constant.29.clone.taps_ref, bf16[32,256,256]{2,1,0:T(8,128)(2,1)} %fusion.high_ref, bf16[32,256,256]{2,1,0:T(8,128)(2,1)} %subtract_convert_fusion.low_ref), custom_call_target="tpu_custom_call" | custom-call | flops 19327352832 | bytes 50331648 | tf_op jit(solution)/shard_map/pallas_call | solution.py:190
  115.1 0.0 collective-permute-done.prev_ref
  115.1 27.2 %shard_map.92.refs_0_ = bf16[32,2,4,32,16,128]{5,4,3,2,1,0:T(8,128)(2,1)} custom-call(bf16[2,64,131072]{2,1,0:T(8,128)(2,1)} %x_ref.3, bf16[2,64,12288]{2,1,0:T(8,128)(2,1)} %collective-permute-done.prev_ref, f32[4,32,128]{2,1,0:T(8,128)} %constant.29.clone.taps_ref, bf16[32,256,256]{2,1,0:T(8,128)(2,1)} %fusion.high_ref, ...), custom_call_target="tpu_custom_call", output_to_operand_aliasing={{}: (5, {})} | custom-call | flops 6442450944 | bytes 16777216 | tf_op jit(solution)/shard_map/pallas_call | solution.py:190
  142.3 0.0 all-gather.2.cloned.1.call-done
  142.3 3.9 copy.46
  146.2 3.8 copy.47
  149.9 1.5 slice_bitcast_fusion
  151.4 252.9 %shard_map.93 = bf16[8,4,2,64,128]{4,3,2,1,0:T(8,128)(2,1)} custom-call(bf16[32,2,4,32,16,128]{5,4,3,2,1,0:T(8,128)(2,1)} %shard_map.92.refs_0_, f32[32,64,128]{2,1,0:T(8,128)} %get-tuple-element.6.refs_1_, f32[32,64,128]{2,1,0:T(8,128)} %get-tuple-element.5.refs_2_), custom_call_target="tpu_custom_call" | custom-call | tf_op jit(solution)/shard_map/pallas_call | solution.py:548
  404.3 1.6 constant_dynamic-slice_fusion
  405.9 0.9 copy.53
  406.8 0.5 copy.59
  407.4 0.4 reshape.30
  407.8 12.2 %all_to_all.27 = bf16[8,2,8192]{2,1,0:T(2,128)(2,1)S(1)} all-to-all(bf16[8,2,8192]{2,1,0:T(2,128)(2,1)S(1)} %reshape.30), channel_id=1, replica_groups=mesh['section'=4,'chan'=8] {'chan'}, dimensions={0} | all-to-all | bytes 524288 | tf_op jit(solution)/shard_map/all_to_all | solution.py:581
  420.0 0.3 reshape.31
  420.4 0.4 copy.50
  420.8 0.1 multiply_reduce_fusion
  420.9 0.1 copy.55
  421.0 0.1 copy.51
  421.1 0.1 bitcast_divide_fusion
  421.2 1.0 copy.52
  (5 shorter events, 0.1 us)
Async XLA Ops:
  8.7 16.6 %copy-start = (f32[128,128]{1,0:T(8,128)S(1)}, f32[128,128]{1,0:T(8,128)}, u32[]{:S(2)}) copy-start(f32[128,128]{1,0:T(8,128)} %constant.27.clone) | copy-start | bytes 196612
  8.7 16.6 %copy-start.1 = (f32[128,128]{1,0:T(8,128)S(1)}, f32[128,128]{1,0:T(8,128)}, u32[]{:S(2)}) copy-start(f32[128,128]{1,0:T(8,128)} %constant.28.clone) | copy-start | bytes 196612
  8.7 16.6 %copy-start.2 = (f32[32,128]{1,0:T(8,128)S(1)}, f32[32,128]{1,0:T(8,128)}, u32[]{:S(2)}) copy-start(f32[32,128]{1,0:T(8,128)} %constant.25.clone) | copy-start | bytes 49156
  8.8 16.6 %copy-start.3 = (f32[32,128]{1,0:T(8,128)S(1)}, f32[32,128]{1,0:T(8,128)}, u32[]{:S(2)}) copy-start(f32[32,128]{1,0:T(8,128)} %constant.26.clone) | copy-start | bytes 49156
  10.0 21.7 %all-to-all-start = ((f32[2,128,512]{1,0,2:T(2,128)}), f32[2,128,512]{1,0,2:T(2,128)S(1)}, u32[]{:S(2)}, u32[]{:S(2)}) async-start(f32[2,128,512]{1,0,2:T(2,128)} %pad_maximum_fusion), calls=%async_computation | async-start | bytes 1048576 | tf_op jit(solution)/shard_map/all_to_all | solution.py:567
  16.4 125.9 %all-gather.2.cloned.1.call-start = ((), (), s32[]{:S(2)}) async-start(), calls=%async_computation.2 | async-start | bytes 2621440 | tf_op jit(solution)/shard_map/all_gather | solution.py:568
  20.3 94.8 %collective-permute-start = (bf16[2,64,12288]{2,1,0:T(8,128)(2,1)}, bf16[2,64,12288]{2,1,0:T(8,128)(2,1)}, u32[]{:S(2)}, u32[]{:S(2)}) collective-permute-start(bf16[2,64,12288]{2,1,0:T(8,128)(2,1)} %slice.9), channel_id=1, source_target_pairs={{0,8},{8,16},{16,24},{1,9},{9,17},{17,25},{2,10},{10,18},{18,26},{... | collective-permute-start | bytes 9437192 | tf_op jit(solution)/shard_map/ppermute | solution.py:564
Sparse Core Ops, SparseCore 0:
  32.8 50.9 all-gather.1

commit v2 on v1

--- a/solution.py
+++ b/solution.py
@@ -29,19 +29,12 @@
     return taps.astype(np.float32).reshape(TAPS, OUTER, LANES)
 
 
-def second_table():
+def table_seed():
     j = np.arange(LANES)
-    twist = np.exp(-2j * np.pi * (np.outer(np.arange(OUTER), j) % CHANNELS) / CHANNELS)
     inner = np.exp(-2j * np.pi * (np.outer(j, j) % LANES) / LANES) / math.sqrt(CHANNELS)
-    tr, ti = (jnp.asarray(a.astype(np.float32))[:, :, None] for a in (twist.real, twist.imag))
-    fr, fi = (jnp.asarray(a.astype(np.float32))[None] for a in (inner.real, inner.imag))
-    re, im = tr * fr - ti * fi, tr * fi + ti * fr
-    table = jnp.concatenate(
-        [jnp.concatenate([re, im], axis=2), jnp.concatenate([-im, re], axis=2)], axis=1
-    )
-    high = table.astype(BF16)
-    low = (table - lax.optimization_barrier(high).astype(F32)).astype(BF16)
-    return high, low
+    twist = np.exp(-2j * np.pi * np.repeat(j[:, None], LANES, axis=1) / CHANNELS)
+    parts = np.stack([inner.real, inner.imag, twist.real, twist.imag])
+    return jnp.asarray(parts.astype(np.float32))
 
 
 def times(z, w):
@@ -80,31 +73,112 @@
 SLOW = OUTER // QUICK
 
 
-def channelize_kernel(lead, frames, x_ref, prev_ref, taps_ref, high_ref, low_ref, *rest):
-    out_ref, filtered, quick, ah, al, bh, bl = rest[-7:]
+def channelize_kernel(sizes, *refs):
+    frames, tiles, early, n_section = sizes
+    (x_ref, prev_ref, taps_ref, seed_ref, whole_ref, out_ref,
+     filtered, quick, ah, al, bh, bl, high, low, turning, history, send_sem, recv_sem) = refs
     rows = frames * TILE
-
-    def filter_step(m, carry):
-        column = m * LANES
-        taps = [taps_ref[t, pl.ds(m, 1), :] for t in range(TAPS)]
-        for part in range(2):
-            window = []
-            for frame in range(1 - TAPS, frames):
-                if frame < 0:
-                    at = pl.multiple_of((lead + frame) * CHANNELS + column, LANES)
-                    tile = prev_ref[part, :, pl.ds(at, LANES)]
-                else:
-                    at = pl.multiple_of(frame * CHANNELS + column, LANES)
-                    tile = x_ref[part, :, pl.ds(at, LANES)]
-                window.append(tile.astype(F32))
-            for b in range(frames):
-                total = window[b] * taps[0]
-                for t in range(1, TAPS):
-                    total = total + window[b + t] * taps[t]
-                filtered[m, part, b * TILE : (b + 1) * TILE, :] = total
-        return carry
-
-    lax.fori_loop(0, OUTER, filter_step, 0)
+    margin = (TAPS - 1) * CHANNELS
+    step = pl.program_id(0)
+    last = pl.num_programs(0) - 1
+    me = lax.axis_index("section")
+
+    def history_copy(tile):
+        start = whole_ref.shape[2] - margin
+        src = whole_ref.at[:, pl.ds(tile * TILE, TILE), pl.ds(start, margin)]
+        return pltpu.make_async_remote_copy(
+            src_ref=src, dst_ref=history.at[tile], send_sem=send_sem.at[tile],
+            recv_sem=recv_sem.at[tile], device_id={"section": (me + 1) % n_section},
+            device_id_type=pl.DeviceIdType.MESH,
+        )
+
+    @pl.when(step == 0)
+    def _():
+        barrier = pltpu.get_barrier_semaphore()
+        for to in ((me + 1) % n_section, (me + n_section - 1) % n_section):
+            pl.semaphore_signal(barrier, inc=1, device_id={"section": to},
+                                device_id_type=pl.DeviceIdType.MESH)
+        pl.semaphore_wait(barrier, 2)
+
+        @pl.when(me < n_section - 1)
+        def _():
+            for tile in range(tiles):
+                history_copy(tile).start()
+
+        @pl.when(me == 0)
+        def _():
+            def clear(i, carry):
+                at = pl.ds(pl.multiple_of(i * LANES, LANES), LANES)
+                for tile in range(tiles):
+                    for part in range(2):
+                        history[tile, part, :, at] = jnp.zeros((TILE, LANES), BF16)
+                return carry
+
+            lax.fori_loop(0, margin // LANES, clear, 0)
+
+        turning[...] = seed_ref[0:2]
+
+        def build(k1, carry):
+            for r in range(0, LANES, TILE):
+                at = slice(r, r + TILE)
+                below = slice(LANES + r, LANES + r + TILE)
+                re, im = turning[0, at, :], turning[1, at, :]
+                for rows_at, left, value in ((at, 0, re), (at, LANES, im),
+                                             (below, 0, -im), (below, LANES, re)):
+                    top = value.astype(BF16)
+                    columns = slice(left, left + LANES)
+                    high[k1, rows_at, columns] = top
+                    low[k1, rows_at, columns] = (value - top.astype(F32)).astype(BF16)
+                tr, ti = seed_ref[2, at, :], seed_ref[3, at, :]
+                turning[0, at, :] = re * tr - im * ti
+                turning[1, at, :] = re * ti + im * tr
+            return carry
+
+        lax.fori_loop(0, OUTER, build, 0)
+
+    def run_filter(before):
+        def filter_step(m, carry):
+            column = m * LANES
+            taps = [taps_ref[t, pl.ds(m, 1), :] for t in range(TAPS)]
+            for part in range(2):
+                window = []
+                for frame in range(1 - TAPS, frames):
+                    if frame < 0:
+                        tile = before(frame, part, column)
+                    else:
+                        at = pl.multiple_of(frame * CHANNELS + column, LANES)
+                        tile = x_ref[part, :, pl.ds(at, LANES)]
+                    window.append(tile.astype(F32))
+                for b in range(frames):
+                    total = window[b] * taps[0]
+                    for t in range(1, TAPS):
+                        total = total + window[b + t] * taps[t]
+                    filtered[m, part, b * TILE : (b + 1) * TILE, :] = total
+            return carry
+
+        lax.fori_loop(0, OUTER, filter_step, 0)
+
+    @pl.when(step < early)
+    def _():
+        def before(frame, part, column):
+            at = pl.multiple_of((4 + frame) * CHANNELS + column, LANES)
+            return prev_ref[part, :, pl.ds(at, LANES)]
+
+        run_filter(before)
+
+    @pl.when(step >= early)
+    def _():
+        tile = step - early
+
+        @pl.when(me > 0)
+        def _():
+            history_copy(tile).wait_recv()
+
+        def before(frame, part, column):
+            at = pl.multiple_of((TAPS - 1 + frame) * CHANNELS + column, LANES)
+            return history[tile, part, :, pl.ds(at, LANES)]
+
+        run_filter(before)
 
     def quick_step(r, carry):
         at = pl.ds(pl.multiple_of(r * 8, 8), 8)
@@ -131,14 +205,15 @@
                 for part in range(2):
                     hi = z[part].astype(BF16)
                     lo = (z[part] - hi.astype(F32)).astype(BF16)
-                    hi_ref[i, at, part * LANES : (part + 1) * LANES] = hi
-                    lo_ref[i, at, part * LANES : (part + 1) * LANES] = lo
+                    hi_ref[i, part, at, :] = hi
+                    lo_ref[i, part, at, :] = lo
 
     def matmul_step(k, hi_ref, lo_ref):
         for i in range(SLOW):
             k1 = i * QUICK + k
-            hi, lo = hi_ref[i], lo_ref[i]
-            th, tl = high_ref[k1], low_ref[k1]
+            hi = jnp.concatenate([hi_ref[i, 0], hi_ref[i, 1]], axis=1)
+            lo = jnp.concatenate([lo_ref[i, 0], lo_ref[i, 1]], axis=1)
+            th, tl = high[k1], low[k1]
             dot = functools.partial(jnp.dot, preferred_element_type=F32)
             res = (dot(hi, th) + dot(lo, th)) + dot(hi, tl)
             for part in range(2):
@@ -157,61 +232,66 @@
 
     lax.fori_loop(0, QUICK // 2, pair_step, 0)
 
-
-def channelize(voltages, before, high, low, earlier):
+    @pl.when((step == last) & (me < n_section - 1))
+    def _():
+        for tile in range(tiles):
+            history_copy(tile).wait_send()
+
+
+def channelize(voltages, n_section):
     feeds_here = voltages.shape[1]
     blocks = voltages.shape[2] // CHANNELS
     frames = 8
-    first = 0 if before is not None else 1
-    steps = 1 if before is not None else blocks // frames - 1
-    lead = TAPS - 1 if before is not None else 4
-    if before is None:
-        before = voltages
+    tiles, groups = feeds_here // TILE, blocks // frames
+    early = tiles * (groups - 1)
+    rows = frames * TILE
     per = frames // 4
-    if lead == 4:
-        before_map = lambda f, b: (0, f, (b + first) * per - 1)
-    else:
-        before_map = lambda f, b: (0, f, 0)
-    in_specs = [
-        pl.BlockSpec((2, TILE, frames * CHANNELS), lambda f, b: (0, f, b + first)),
-        pl.BlockSpec((2, TILE, lead * CHANNELS), before_map),
-        pl.BlockSpec((TAPS, OUTER, LANES), lambda f, b: (0, 0, 0)),
-        pl.BlockSpec((OUTER, 2 * LANES, 2 * LANES), lambda f, b: (0, 0, 0)),
-        pl.BlockSpec((OUTER, 2 * LANES, 2 * LANES), lambda f, b: (0, 0, 0)),
-    ]
-    args = [voltages, before, jnp.asarray(prototype()), high, low]
-    aliases = {}
-    if earlier is not None:
-        in_specs.append(pl.BlockSpec(memory_space=pl.ANY))
-        args.append(earlier)
-        aliases = {5: 0}
-    rows = frames * TILE
-    share = steps * frames * feeds_here
+
+    def place(i):
+        late = i >= early
+        tile = jnp.where(late, i - early, i // (groups - 1))
+        return tile, jnp.where(late, 0, 1 + i % (groups - 1))
+
+    def x_map(i):
+        tile, group = place(i)
+        return 0, tile, group
+
+    def prev_map(i):
+        tile, group = place(jnp.minimum(i, early - 1))
+        return 0, tile, group * per - 1
+
+    def out_map(i):
+        tile, group = place(i)
+        return 0, 0, tile, group, 0, 0
+
+    table = pltpu.VMEM((OUTER, 2 * LANES, 2 * LANES), BF16)
+    half = pltpu.VMEM((SLOW, 2, rows, LANES), BF16)
     return pl.pallas_call(
-        functools.partial(channelize_kernel, lead, frames),
-        grid=(feeds_here // TILE, steps),
-        in_specs=in_specs,
-        out_specs=pl.BlockSpec(
-            (OUTER, 2, 1, frames, TILE, LANES), lambda f, b: (0, 0, f, b + first, 0, 0)
-        ),
-        out_shape=jax.ShapeDtypeStruct(
-            (OUTER, 2, feeds_here // TILE, blocks, TILE, LANES), BF16
-        ),
+        functools.partial(channelize_kernel, (frames, tiles, early, n_section)),
+        grid=(tiles * groups,),
+        in_specs=[
+            pl.BlockSpec((2, TILE, frames * CHANNELS), x_map),
+            pl.BlockSpec((2, TILE, 4 * CHANNELS), prev_map),
+            pl.BlockSpec((TAPS, OUTER, LANES), lambda i: (0, 0, 0)),
+            pl.BlockSpec((4, LANES, LANES), lambda i: (0, 0, 0)),
+            pl.BlockSpec(memory_space=pl.ANY),
+        ],
+        out_specs=pl.BlockSpec((OUTER, 2, 1, frames, TILE, LANES), out_map),
+        out_shape=jax.ShapeDtypeStruct((OUTER, 2, tiles, blocks, TILE, LANES), BF16),
         scratch_shapes=[
             pltpu.VMEM((OUTER, 2, rows, LANES), F32),
             pltpu.VMEM((QUICK, SLOW, 2, rows, LANES), F32),
-        ]
-        + [pltpu.VMEM((SLOW, rows, 2 * LANES), BF16)] * 4,
-        input_output_aliases=aliases,
+            half, half, half, half, table, table,
+            pltpu.VMEM((2, LANES, LANES), F32),
+            pltpu.VMEM((tiles, 2, TILE, (TAPS - 1) * CHANNELS), BF16),
+            pltpu.SemaphoreType.DMA((tiles,)),
+            pltpu.SemaphoreType.DMA((tiles,)),
+        ],
         compiler_params=pltpu.CompilerParams(
-            dimension_semantics=("arbitrary", "arbitrary"), vmem_limit_bytes=VMEM_LIMIT
+            dimension_semantics=("arbitrary",), vmem_limit_bytes=VMEM_LIMIT,
+            collective_id=0, has_side_effects=True,
         ),
-        cost_estimate=pl.CostEstimate(
-            flops=share * CHANNELS * 2 * 256 * 6,
-            bytes_accessed=share * CHANNELS * 8,
-            transcendentals=0,
-        ),
-    )(*args)
+    )(voltages, voltages, jnp.asarray(prototype()), table_seed(), voltages)
 
 
 def fold_rows(parts):
@@ -238,7 +318,7 @@
 
 def solve_kernel(sizes, *refs):
     n_section, n_chan, feeds, blocks, chunks, kc = sizes
-    (spectra_hbm, weight_ref, power_ref, out_ref,
+    (spectra_hbm, power_ref, out_ref,
      spectra, diagonal, local_p, half_in, half_sum, piece_in, full_p, scaled,
      norm, local_q, q_in, y_ref,
      load_sem, half_ss, half_rs, piece_ss, piece_rs, gather_ss, gather_rs,
@@ -319,10 +399,48 @@
     def pair(k1, tile, b):
         return spectra[k1, 0, tile, b].astype(F32), spectra[k1, 1, tile, b].astype(F32)
 
+    def store_rows(c, k, g, rows_r, rows_i):
+        at = (k % half_k) * (2 * blocks) + g * 8
+        h = k // half_k
+        local_p[c, h, pl.ds(pl.multiple_of(at, 8), 8), :] = fold_rows(rows_r)
+        at = at + blocks
+        local_p[c, h, pl.ds(pl.multiple_of(at, 8), 8), :] = fold_rows(rows_i)
+
     def project(it, c):
         @pl.when(it == 0)
         def _():
             load(c).wait()
+
+            def one(k, carry):
+                k1 = c * kc + k
+                power = [power_ref[k1, t * TILE : (t + 1) * TILE, :].astype(F32)
+                         for t in range(tiles)]
+                weight = [jnp.where(p > 0, 1.0, 0.0) for p in power]
+
+                def group(g, totals):
+                    totals = list(totals)
+                    rows_r, rows_i = [], []
+                    for s in range(8):
+                        b = g * 8 + s
+                        ar = ai = jnp.zeros((TILE, LANES), F32)
+                        for t in range(tiles):
+                            re, im = pair(k1, t, b)
+                            ar = ar + re * weight[t]
+                            ai = ai - im * weight[t]
+                            totals[t] = totals[t] + (re * re + im * im)
+                        rows_r.append(ar[:8] + ar[8:])
+                        rows_i.append(ai[:8] + ai[8:])
+                    store_rows(c, k, g, rows_r, rows_i)
+                    return tuple(totals)
+
+                zero = jnp.zeros((TILE, LANES), F32)
+                totals = lax.fori_loop(0, blocks // 8, group, (zero,) * tiles)
+                for t in range(tiles):
+                    at = slice(t * TILE, (t + 1) * TILE)
+                    diagonal[k1, at, :] = blocks * power[t] - totals[t]
+                return carry
+
+            lax.fori_loop(0, kc, one, 0)
 
         @pl.when(it > 0)
         def _():
@@ -331,61 +449,37 @@
             for copy in y_copies(c, receive=True):
                 copy.wait_recv()
 
-        def one(k, carry):
-            k1 = c * kc + k
-            yr = [y_ref[c, k, 0, t * TILE : (t + 1) * TILE, :].astype(F32) for t in range(tiles)]
-            yi = [y_ref[c, k, 1, t * TILE : (t + 1) * TILE, :].astype(F32) for t in range(tiles)]
-            square = sum(a * a for a in yr + yi)
-            norm[c, 0, pl.ds(k, 1), :] = jnp.sum(square, axis=0, keepdims=True)
-
-            def group(g, carry):
-                rows_r, rows_i = [], []
-                for s in range(8):
-                    b = g * 8 + s
-                    ar = ai = None
-                    for t in range(tiles):
-                        re, im = pair(k1, t, b)
-                        pr = re * yr[t] + im * yi[t]
-                        pi = re * yi[t] - im * yr[t]
-                        ar = pr if ar is None else ar + pr
-                        ai = pi if ai is None else ai + pi
-                    rows_r.append(ar[:8] + ar[8:])
-                    rows_i.append(ai[:8] + ai[8:])
-                at = (k % half_k) * (2 * blocks) + g * 8
-                h = k // half_k
-                local_p[c, h, pl.ds(pl.multiple_of(at, 8), 8), :] = fold_rows(rows_r)
-                at = at + blocks
-                local_p[c, h, pl.ds(pl.multiple_of(at, 8), 8), :] = fold_rows(rows_i)
+            def one(k, carry):
+                k1 = c * kc + k
+                yr, yi = ([y_ref[c, k, part, t * TILE : (t + 1) * TILE, :].astype(F32)
+                           for t in range(tiles)] for part in range(2))
+                square = sum(a * a for a in yr + yi)
+                norm[c, 0, pl.ds(k, 1), :] = jnp.sum(square, axis=0, keepdims=True)
+
+                def group(g, carry):
+                    rows_r, rows_i = [], []
+                    for s in range(8):
+                        b = g * 8 + s
+                        ar = ai = None
+                        for t in range(tiles):
+                            re, im = pair(k1, t, b)
+                            pr = re * yr[t] + im * yi[t]
+                            pi = re * yi[t] - im * yr[t]
+                            ar = pr if ar is None else ar + pr
+                            ai = pi if ai is None else ai + pi
+                        rows_r.append(ar[:8] + ar[8:])
+                        rows_i.append(ai[:8] + ai[8:])
+                    store_rows(c, k, g, rows_r, rows_i)
+                    return carry
+
+                lax.fori_loop(0, blocks // 8, group, 0)
                 return carry
 
-            lax.fori_loop(0, blocks // 8, group, 0)
-            return carry
-
-        lax.fori_loop(0, kc, one, 0)
+            lax.fori_loop(0, kc, one, 0)
+
         half_copy(c).start()
         for copy in norm_copies(c):
             copy.start()
-
-        @pl.when(it == 0)
-        def _():
-            def one_d(k, carry):
-                k1 = c * kc + k
-
-                def step(b, totals):
-                    new = []
-                    for t in range(tiles):
-                        re, im = pair(k1, t, b)
-                        new.append(totals[t] + (re * re + im * im))
-                    return tuple(new)
-
-                zero = jnp.zeros((TILE, LANES), F32)
-                totals = lax.fori_loop(0, blocks, step, (zero,) * tiles)
-                for t in range(tiles):
-                    at = slice(t * TILE, (t + 1) * TILE)
-                    diagonal[k1, at, :] = blocks * power_ref[k1, at, :] - totals[t]
-                return carry
-
-            lax.fori_loop(0, kc, one_d, 0)
 
     def add_half(it, c):
         half_copy(c).wait()
@@ -431,8 +525,8 @@
 
             def group(g, totals):
                 totals = list(totals)
-                for s in range(4):
-                    b = g * 4 + s
+                for s in range(8):
+                    b = g * 8 + s
                     pr = scaled[pl.ds(b, 1), :]
                     pi = scaled[pl.ds(blocks + b, 1), :]
                     for t in range(tiles):
@@ -442,14 +536,14 @@
                 return tuple(totals)
 
             zero = jnp.zeros((TILE, LANES), F32)
-            totals = lax.fori_loop(0, blocks // 4, group, (zero,) * (2 * tiles))
+            totals = lax.fori_loop(0, blocks // 8, group, (zero,) * (2 * tiles))
             for t in range(tiles):
                 at = slice(t * TILE, (t + 1) * TILE)
-                weight = weight_ref[k1, at, :]
+                usable = power_ref[k1, at, :].astype(F32) > 0
                 shift = diagonal[k1, at, :] * inv
                 for part in range(2):
                     now = y_ref[c, k, part, at, :].astype(F32)
-                    value = weight * (totals[2 * t + part] + shift * now)
+                    value = jnp.where(usable, totals[2 * t + part] + shift * now, 0.0)
                     local_q[c, k, part, at, :] = value.astype(BF16)
             return carry
 
@@ -485,18 +579,21 @@
     @pl.loop(0, chunks)
     def _(c):
         for k in range(kc):
-            y_ref[c, k, 0] = weight_ref[c * kc + k].astype(BF16)
+            power = power_ref[c * kc + k].astype(F32)
+            y_ref[c, k, 0] = jnp.where(power > 0, 1.0, 0.0).astype(BF16)
             y_ref[c, k, 1] = jnp.zeros((feeds, LANES), BF16)
         norm[c, 0] = jnp.zeros((8, LANES), F32)
 
     pl.semaphore_wait(barrier, n_chan + n_section - 2)
 
-    stages = [project, add_half, add_pieces, share_half, expand, add_sections]
-    period = max(chunks, len(stages) + 1)
-
-    @pl.loop(0, ITERS * period + len(stages))
+    stages = [(7, add_sections), (3, add_pieces), (5, expand), (4, share_half), (1, add_half),
+              (0, project)]
+    span = 7
+    period = max(chunks, span + 1)
+
+    @pl.loop(0, ITERS * period + span)
     def _(slot):
-        for lag, stage in reversed(list(enumerate(stages))):
+        for lag, stage in stages:
             turn = slot - lag + period
             it, c = turn // period - 1, turn % period
 
@@ -514,7 +611,7 @@
     out_ref[...] = y_ref[...]
 
 
-def solve(spectra, weight, power, n_section, n_chan):
+def solve(spectra, power, n_section, n_chan):
     feeds, blocks = spectra.shape[2] * TILE, spectra.shape[3]
     kc = n_section
     chunks = OUTER // kc
@@ -547,33 +644,26 @@
     vmem = pl.BlockSpec(memory_space=pltpu.VMEM)
     return pl.pallas_call(
         functools.partial(solve_kernel, (n_section, n_chan, feeds, blocks, chunks, kc)),
-        in_specs=[pl.BlockSpec(memory_space=pl.ANY), vmem, vmem],
+        in_specs=[pl.BlockSpec(memory_space=pl.ANY), vmem],
         out_specs=vmem,
         out_shape=jax.ShapeDtypeStruct((chunks, kc, 2, feeds, LANES), BF16),
         scratch_shapes=scratch,
         compiler_params=pltpu.CompilerParams(
             collective_id=1, has_side_effects=True, vmem_limit_bytes=VMEM_LIMIT
         ),
-    )(spectra, weight, power)
+    )(spectra, power)
 
 
 def local(voltages, usable, auto_power):
     n_section, n_chan = lax.axis_size("section"), lax.axis_size("chan")
-    margin = (TAPS - 1) * CHANNELS
-    tail = voltages[:, :, voltages.shape[2] - margin :]
-    history = lax.ppermute(tail, "section", [(i, i + 1) for i in range(n_section - 1)])
-
-    small = jnp.stack([usable.astype(F32), auto_power], axis=0)
-    small = lax.all_to_all(small, "chan", split_axis=2, concat_axis=1, tiled=True)
-    small = lax.all_gather(small, "section", axis=1, tiled=True)
-    feeds_here = small.shape[2]
-    small = small.reshape(2, LANES, OUTER, feeds_here).transpose(0, 2, 3, 1)
-
-    high, low = second_table()
-    spectra = channelize(voltages, None, high, low, None)
-    spectra = channelize(voltages, history, high, low, spectra)
-
-    result = solve(spectra, small[0], small[1], n_section, n_chan)
+    power = (usable.astype(F32) * auto_power).astype(BF16)
+    power = lax.all_to_all(power, "chan", split_axis=1, concat_axis=0, tiled=True)
+    power = lax.all_gather(power, "section", axis=0, tiled=True)
+    feeds_here = power.shape[1]
+    power = power.reshape(LANES, OUTER, feeds_here).transpose(1, 2, 0)
+
+    spectra = channelize(voltages, n_section)
+    result = solve(spectra, power, n_section, n_chan)
     result = result.reshape(OUTER, 2, feeds_here, LANES)
     width = LANES // n_section
     result = lax.dynamic_slice_in_dim(result, lax.axis_index("section") * width, width, axis=3)

time: 429 us -> 302 us (0.70)
  Pallas kernels: 351 us -> 262 us
  other arithmetic: 15.5 us -> 0.88 us
  between operations: 13.6 us -> 0.13 us
  local copies, waits for them, and re-layouts: 21.4 us -> 9.88 us
  blocking collectives: 12.2 us -> 22.3 us
  starting transfers between devices: 11.4 us -> 6.35 us
    pallas_call x1, Pallas kernels: 253 us -> 170 us  [solve(): pl.pallas_call(functools.partial(solve_kernel, (n_section, n_chan, feeds,...]
    convert_element_type x3 -> x1, other arithmetic: 11.4 us -> 0.69 us  [local(): power = (usable.astype(F32) * auto_power).astype(BF16)]
    all_gather x0 -> x1, blocking collectives: none -> 9.03 us  [local(): power = lax.all_gather(power, 'section', axis=0, tiled=True)]
    pallas_call x2 -> x1, Pallas kernels: 98.3 us -> 92.4 us  [channelize(): pl.pallas_call(functools.partial(channelize_kernel, (frames, tiles, early...]
    ppermute x1 -> x0, starting transfers between devices: 5.05 us -> none  [local(): lax.ppermute(tail, 'section', [(i, i + 1) for i in range(n_section - 1)])]
  transfers between devices with their start and end apart: 3 -> 1, of which waited for: 1 -> 0; matrix products, arithmetic and copies ran while one was open for 4% -> 0% of each run, Pallas kernels for 23% -> 31%
where the time goes in v2:
time: 302 us
  Pallas kernels  262 us (87%)
  blocking collectives  22.3 us (7%)
  local copies, waits for them, and re-layouts  9.88 us (3%)
  starting transfers between devices  6.35 us (2%)
    pallas_call x1, Pallas kernels, solve(): pl.pallas_call(functools.partial(solve_kernel, (n_section, n_chan, feeds,...  170 us
    pallas_call x1, Pallas kernels, channelize(): pl.pallas_call(functools.partial(channelize_kernel, (frames, tiles, early...  92.4 us
    all_to_all x1, blocking collectives, local(): lax.all_to_all(result, 'chan', split_axis=1, concat_axis=2, tiled=True)  13.3 us
    all_gather x1, blocking collectives, local(): power = lax.all_gather(power, 'section', axis=0, tiled=True)  9.03 us
    all_to_all x1, starting transfers between devices, local(): lax.all_to_all(power, 'chan', split_axis=1, concat_axis=0, tiled=True)  6.35 us
  transfers between devices with their start and end apart: 1, of which 0 were waited for; matrix products, arithmetic and copies ran while one was open for 0% of the time, Pallas kernels for 31%

profile of v2, /device:TPU:0, one launch (start us, length us, event | category | flops | bytes accessed | tf_op | source)
XLA Modules:
  0.0 301.9 jit_solution(15966232662967686122)
XLA Ops:
  0.0 1.1 copy.36
  1.1 1.1 copy.35
  2.2 0.7 multiply_convert_fusion
  2.9 6.4 %all-to-all-start = ((bf16[128,8,64]{0,2,1:T(8,128)(2,1)}), bf16[128,8,64]{0,2,1:T(8,128)(2,1)S(1)}, u32[]{:S(2)}, u32[]{:S(2)}) async-start(bf16[128,8,64]{0,2,1:T(8,128)(2,1)} %bitcast), calls=%async_computation | async-start | bytes 262144 | tf_op jit(solution)/shard_map/all_to_all | solution.py:660
  9.2 92.4 %shard_map.55.refs_0_ = bf16[32,2,4,32,16,128]{5,4,3,2,1,0:T(8,128)(2,1)} custom-call(bf16[2,64,131072]{2,1,0:T(8,128)(2,1)} %refs_4_.1, bf16[2,64,131072]{2,1,0:T(8,128)(2,1)} %refs_4_.1, f32[4,32,128]{2,1,0:T(8,128)} %constant.19.clone.refs_2_, f32[4,128,128]{2,1,0:T(8,128)} %constant.20.clone.refs_3_, bf16[2,64,131072]{2,1,0:T(8,128)(2,1)} %refs_4_.1), custom_call_target="tpu_custom_call" | custom-call | tf_op jit(solution)/shard_map/pallas_call | solution.py:269
  101.6 0.0 all-to-all-done
  101.7 9.0 %all_gather.3 = bf16[4096,64]{0,1:T(8,128)(2,1)S(1)} all-gather(bf16[1024,64]{0,1:T(8,128)(2,1)S(1)} %copy_bitcast_fusion), channel_id=1, replica_groups=mesh['section'=4,'chan'=8] {'section'}, dimensions={0}, use_global_device_ids=true | all-gather | bytes 655360 | tf_op jit(solution)/shard_map/all_gather | solution.py:661
  110.7 0.5 copy.38
  111.2 1.9 copy.39
  113.1 169.9 %shard_map.56 = bf16[8,4,2,64,128]{4,3,2,1,0:T(8,128)(2,1)} custom-call(bf16[32,2,4,32,16,128]{5,4,3,2,1,0:T(8,128)(2,1)} %shard_map.55.refs_0_, bf16[32,64,128]{2,1,0:T(8,128)(2,1)} %bitcast.31), custom_call_target="tpu_custom_call" | custom-call | tf_op jit(solution)/shard_map/pallas_call | solution.py:645
  282.9 1.6 constant_dynamic-slice_fusion
  284.6 0.9 copy.45
  285.5 0.5 copy.50
  286.0 0.4 reshape.29
  286.4 13.3 %all_to_all.28 = bf16[8,2,8192]{2,1,0:T(2,128)(2,1)S(1)} all-to-all(bf16[8,2,8192]{2,1,0:T(2,128)(2,1)S(1)} %reshape.29), channel_id=1, replica_groups=mesh['section'=4,'chan'=8] {'chan'}, dimensions={0} | all-to-all | bytes 524288 | tf_op jit(solution)/shard_map/all_to_all | solution.py:671
  299.7 0.3 reshape.30
  300.1 0.4 copy.42
  300.5 0.1 multiply_reduce_fusion
  300.6 0.1 copy.47
  300.7 0.1 copy.43
  300.8 0.1 bitcast_divide_fusion
  300.9 1.0 copy.44
  (4 shorter events, 0.1 us)
Async XLA Ops:
  2.9 98.8 %all-to-all-start = ((bf16[128,8,64]{0,2,1:T(8,128)(2,1)}), bf16[128,8,64]{0,2,1:T(8,128)(2,1)S(1)}, u32[]{:S(2)}, u32[]{:S(2)}) async-start(bf16[128,8,64]{0,2,1:T(8,128)(2,1)} %bitcast), calls=%async_computation | async-start | bytes 262144 | tf_op jit(solution)/shard_map/all_to_all | solution.py:660

commit v3 on v2

--- a/solution.py
+++ b/solution.py
@@ -74,14 +74,30 @@
 
 
 def channelize_kernel(sizes, *refs):
-    frames, tiles, early, n_section = sizes
-    (x_ref, prev_ref, taps_ref, seed_ref, whole_ref, out_ref,
-     filtered, quick, ah, al, bh, bl, high, low, turning, history, send_sem, recv_sem) = refs
+    frames, tiles, early, n_section, n_chan = sizes
+    (x_ref, prev_ref, taps_ref, seed_ref, whole_ref, power_ref, out_ref, all_power,
+     filtered, quick, ah, al, bh, bl, high, low, turning, history, send_sem, recv_sem, power_ss, power_rs, own_sem) = refs
     rows = frames * TILE
     margin = (TAPS - 1) * CHANNELS
     step = pl.program_id(0)
     last = pl.num_programs(0) - 1
     me = lax.axis_index("section")
+    n_dev = n_section * n_chan
+    place = me * n_chan + lax.axis_index("chan")
+
+    def power_copy(d, receive=False):
+        to = (place + d) % n_dev
+        owner = (place - d + n_dev) % n_dev if receive else place
+        return pltpu.make_async_remote_copy(
+            src_ref=power_ref.at[to % n_chan], dst_ref=all_power.at[owner],
+            send_sem=power_ss.at[d - 1], recv_sem=power_rs.at[d - 1],
+            device_id={"section": to // n_chan, "chan": to % n_chan},
+            device_id_type=pl.DeviceIdType.MESH,
+        )
+
+    own_power = pltpu.make_async_copy(
+        power_ref.at[place % n_chan], all_power.at[place], own_sem
+    )
 
     def history_copy(tile):
         start = whole_ref.shape[2] - margin
@@ -95,15 +111,26 @@
     @pl.when(step == 0)
     def _():
         barrier = pltpu.get_barrier_semaphore()
-        for to in ((me + 1) % n_section, (me + n_section - 1) % n_section):
-            pl.semaphore_signal(barrier, inc=1, device_id={"section": to},
+
+        @pl.loop(1, n_dev)
+        def _(d):
+            to = (place + d) % n_dev
+            pl.semaphore_signal(barrier, inc=1,
+                                device_id={"section": to // n_chan, "chan": to % n_chan},
                                 device_id_type=pl.DeviceIdType.MESH)
-        pl.semaphore_wait(barrier, 2)
+
+        pl.semaphore_wait(barrier, n_dev - 1)
 
         @pl.when(me < n_section - 1)
         def _():
             for tile in range(tiles):
                 history_copy(tile).start()
+
+        own_power.start()
+
+        @pl.loop(1, n_dev)
+        def _(d):
+            power_copy(d).start()
 
         @pl.when(me == 0)
         def _():
@@ -237,8 +264,18 @@
         for tile in range(tiles):
             history_copy(tile).wait_send()
 
-
-def channelize(voltages, n_section):
+    @pl.when(step == last)
+    def _():
+        own_power.wait()
+
+        @pl.loop(1, n_dev)
+        def _(d):
+            power_copy(d).wait_send()
+            power_copy(d, receive=True).wait_recv()
+
+
+def channelize(voltages, power, n_section, n_chan):
+    n_dev = n_section * n_chan
     feeds_here = voltages.shape[1]
     blocks = voltages.shape[2] // CHANNELS
     frames = 8
@@ -267,7 +304,7 @@
     table = pltpu.VMEM((OUTER, 2 * LANES, 2 * LANES), BF16)
     half = pltpu.VMEM((SLOW, 2, rows, LANES), BF16)
     return pl.pallas_call(
-        functools.partial(channelize_kernel, (frames, tiles, early, n_section)),
+        functools.partial(channelize_kernel, (frames, tiles, early, n_section, n_chan)),
         grid=(tiles * groups,),
         in_specs=[
             pl.BlockSpec((2, TILE, frames * CHANNELS), x_map),
@@ -275,23 +312,33 @@
             pl.BlockSpec((TAPS, OUTER, LANES), lambda i: (0, 0, 0)),
             pl.BlockSpec((4, LANES, LANES), lambda i: (0, 0, 0)),
             pl.BlockSpec(memory_space=pl.ANY),
+            pl.BlockSpec(memory_space=pl.ANY),
         ],
-        out_specs=pl.BlockSpec((OUTER, 2, 1, frames, TILE, LANES), out_map),
-        out_shape=jax.ShapeDtypeStruct((OUTER, 2, tiles, blocks, TILE, LANES), BF16),
+        out_specs=[
+            pl.BlockSpec((OUTER, 2, 1, frames, TILE, LANES), out_map),
+            pl.BlockSpec(memory_space=pl.ANY),
+        ],
+        out_shape=[
+            jax.ShapeDtypeStruct((OUTER, 2, tiles, blocks, TILE, LANES), BF16),
+            jax.ShapeDtypeStruct((n_dev,) + power.shape[1:], BF16),
+        ],
         scratch_shapes=[
-            pltpu.VMEM((OUTER, 2, rows, LANES), F32),
-            pltpu.VMEM((QUICK, SLOW, 2, rows, LANES), F32),
+            pltpu.VMEM((OUTER, 2, rows + 8, LANES), F32),
+            pltpu.VMEM((QUICK, SLOW, 2, rows + 8, LANES), F32),
             half, half, half, half, table, table,
             pltpu.VMEM((2, LANES, LANES), F32),
             pltpu.VMEM((tiles, 2, TILE, (TAPS - 1) * CHANNELS), BF16),
             pltpu.SemaphoreType.DMA((tiles,)),
             pltpu.SemaphoreType.DMA((tiles,)),
+            pltpu.SemaphoreType.DMA((n_dev - 1,)),
+            pltpu.SemaphoreType.DMA((n_dev - 1,)),
+            pltpu.SemaphoreType.DMA,
         ],
         compiler_params=pltpu.CompilerParams(
             dimension_semantics=("arbitrary",), vmem_limit_bytes=VMEM_LIMIT,
             collective_id=0, has_side_effects=True,
         ),
-    )(voltages, voltages, jnp.asarray(prototype()), table_seed(), voltages)
+    )(voltages, voltages, jnp.asarray(prototype()), table_seed(), voltages, power)
 
 
 def fold_rows(parts):
@@ -319,14 +366,18 @@
 def solve_kernel(sizes, *refs):
     n_section, n_chan, feeds, blocks, chunks, kc = sizes
     (spectra_hbm, power_ref, out_ref,
-     spectra, diagonal, local_p, half_in, half_sum, piece_in, full_p, scaled,
+     spectra, diagonal, local_p, half_in, half_sum, half_out, piece_in, full_p, scaled,
      norm, local_q, q_in, y_ref,
      load_sem, half_ss, half_rs, piece_ss, piece_rs, gather_ss, gather_rs,
-     share_ss, share_rs, norm_ss, norm_rs, q_ss, q_rs, y_ss, y_rs) = refs
+     share_ss, share_rs, norm_ss, norm_rs, q_ss, q_rs, y_ss, y_rs,
+     turned, final_ss, final_rs, own_sem) = refs
     tiles = feeds // TILE
     n_z = n_chan // 2
     me_s = lax.axis_index("section")
     me_c = lax.axis_index("chan")
+    n_dev = n_section * n_chan
+    me = me_s * n_chan + me_c
+    share = LANES // n_dev
     core, z = me_c % 2, me_c // 2
     half_k = kc // 2
     half_rows = half_k * 2 * blocks
@@ -359,7 +410,7 @@
         for d in range(1, n_z):
             to = (z + d) % n_z
             rows = pl.ds(pl.multiple_of(to * piece_rows, piece_rows), piece_rows)
-            copies.append(remote(half_sum.at[c, rows], piece_in.at[c, d - 1],
+            copies.append(remote(half_out.at[c, rows], piece_in.at[c, d - 1],
                                  piece_ss.at[c, d - 1], piece_rs.at[c, d - 1],
                                  chan=to * 2 + core))
         return copies
@@ -456,19 +507,21 @@
                 square = sum(a * a for a in yr + yi)
                 norm[c, 0, pl.ds(k, 1), :] = jnp.sum(square, axis=0, keepdims=True)
 
+                less = [b - a for a, b in zip(yr, yi)]
+                more = [b + a for a, b in zip(yr, yi)]
+
                 def group(g, carry):
                     rows_r, rows_i = [], []
                     for s in range(8):
                         b = g * 8 + s
-                        ar = ai = None
+                        one = two = three = None
                         for t in range(tiles):
                             re, im = pair(k1, t, b)
-                            pr = re * yr[t] + im * yi[t]
-                            pi = re * yi[t] - im * yr[t]
-                            ar = pr if ar is None else ar + pr
-                            ai = pi if ai is None else ai + pi
-                        rows_r.append(ar[:8] + ar[8:])
-                        rows_i.append(ai[:8] + ai[8:])
+                            x, y, z = (re - im) * yr[t], re * less[t], im * more[t]
+                            one, two, three = (x, y, z) if t == 0 else (one + x, two + y, three + z)
+                        one = one[:8] + one[8:]
+                        rows_r.append(one + (three[:8] + three[8:]))
+                        rows_i.append(one + (two[:8] + two[8:]))
                     store_rows(c, k, g, rows_r, rows_i)
                     return carry
 
@@ -483,7 +536,9 @@
 
     def add_half(it, c):
         half_copy(c).wait()
-        half_sum[c] = local_p[c, core] + half_in[c]
+        total = local_p[c, core] + half_in[c]
+        half_sum[c] = total
+        half_out[c] = total.astype(BF16)
         for copy in piece_copies(c):
             copy.start()
 
@@ -493,7 +548,7 @@
         rows = pl.ds(pl.multiple_of(z * piece_rows, piece_rows), piece_rows)
         total = half_sum[c, rows, :]
         for d in range(1, n_z):
-            total = total + piece_in[c, d - 1]
+            total = total + piece_in[c, d - 1].astype(F32)
         full_p[c, core, rows, :] = total
         for copy in gather_copies(c):
             copy.start()
@@ -514,36 +569,41 @@
         for d in range(1, n_chan):
             length = length + norm[c, d]
         inverse = jnp.where(it == 0, 1.0, 1.0 / jnp.sqrt(length + epsilon))
-        norm_scale = scaled.at[pl.ds(2 * blocks, 8)]
-        norm_scale[...] = inverse
+        scaled[pl.ds(3 * blocks, kc), :] = inverse
 
         def one(k, carry):
             k1 = c * kc + k
-            inv = scaled[pl.ds(2 * blocks + k, 1), :]
+            inv = scaled[pl.ds(3 * blocks + k, 1), :]
             at = pl.multiple_of((k % half_k) * (2 * blocks), 2 * blocks)
-            scaled[0 : 2 * blocks, :] = full_p[c, k // half_k, pl.ds(at, 2 * blocks), :] * inv
+            real = full_p[c, k // half_k, pl.ds(at, blocks), :] * inv
+            at = pl.multiple_of(at + blocks, blocks)
+            imag = full_p[c, k // half_k, pl.ds(at, blocks), :] * inv
+            scaled[0:blocks, :] = real
+            scaled[blocks : 2 * blocks, :] = imag - real
+            scaled[2 * blocks : 3 * blocks, :] = imag + real
 
             def group(g, totals):
                 totals = list(totals)
                 for s in range(8):
                     b = g * 8 + s
-                    pr = scaled[pl.ds(b, 1), :]
-                    pi = scaled[pl.ds(blocks + b, 1), :]
+                    pr, less, more = (scaled[pl.ds(i * blocks + b, 1), :] for i in range(3))
                     for t in range(tiles):
                         re, im = pair(k1, t, b)
-                        totals[2 * t] = totals[2 * t] + (re * pr - im * pi)
-                        totals[2 * t + 1] = totals[2 * t + 1] + (re * pi + im * pr)
+                        totals[3 * t] = totals[3 * t] + (re + im) * pr
+                        totals[3 * t + 1] = totals[3 * t + 1] + re * less
+                        totals[3 * t + 2] = totals[3 * t + 2] + im * more
                 return tuple(totals)
 
             zero = jnp.zeros((TILE, LANES), F32)
-            totals = lax.fori_loop(0, blocks // 8, group, (zero,) * (2 * tiles))
+            totals = lax.fori_loop(0, blocks // 8, group, (zero,) * (3 * tiles))
             for t in range(tiles):
                 at = slice(t * TILE, (t + 1) * TILE)
                 usable = power_ref[k1, at, :].astype(F32) > 0
                 shift = diagonal[k1, at, :] * inv
+                sums = totals[3 * t] - totals[3 * t + 2], totals[3 * t] + totals[3 * t + 1]
                 for part in range(2):
                     now = y_ref[c, k, part, at, :].astype(F32)
-                    value = jnp.where(usable, totals[2 * t + part] + shift * now, 0.0)
+                    value = jnp.where(usable, sums[part] + shift * now, 0.0)
                     local_q[c, k, part, at, :] = value.astype(BF16)
             return carry
 
@@ -551,25 +611,59 @@
         for copy in q_copies(c):
             copy.start()
 
+    def final_copy(c, d):
+        to = (me + d) % n_dev
+        return remote(turned.at[c, to], out_ref.at[c, me], final_ss.at[c], final_rs.at[c],
+                      section=to // n_chan, chan=to % n_chan)
+
+    def own_copy(c):
+        return pltpu.make_async_copy(turned.at[c, me], out_ref.at[c, me], own_sem.at[c])
+
+    def final_wait(c):
+        others = turned.at[c, pl.ds(0, n_dev - 1)]
+        pltpu.make_async_copy(others, others, final_ss.at[c]).wait()
+        others = out_ref.at[c, pl.ds(0, n_dev - 1)]
+        pltpu.make_async_copy(others, others, final_rs.at[c]).wait()
+        own_copy(c).wait()
+
+    def section_sum(c, k, part):
+        total = local_q[c, me_s * k_piece + k, part].astype(F32)
+        for d in range(1, n_section):
+            total = total + q_in[c, d - 1, k, part].astype(F32)
+        return total
+
     def add_sections(it, c):
         for copy in q_copies(c):
             copy.wait()
-        for k in range(k_piece):
-            for part in range(2):
-                at = me_s * k_piece + k
-                total = local_q[c, at, part].astype(F32)
-                for d in range(1, n_section):
-                    total = total + q_in[c, d - 1, k, part].astype(F32)
-                y_ref[c, at, part] = total.astype(BF16)
-        for copy in y_copies(c):
-            copy.start()
+
+        @pl.when(it < ITERS - 1)
+        def _():
+            for k in range(k_piece):
+                for part in range(2):
+                    y_ref[c, me_s * k_piece + k, part] = section_sum(c, k, part).astype(BF16)
+            for copy in y_copies(c):
+                copy.start()
+
+        @pl.when(it == ITERS - 1)
+        def _():
+            for k in range(k_piece):
+                parts = [section_sum(c, k, part) for part in range(2)]
+                total = jnp.concatenate(parts, axis=0).T
+                for to in range(n_dev):
+                    turned[c, to, k] = total[to * share : (to + 1) * share]
+            own_copy(c).start()
+
+            @pl.loop(1, n_dev)
+            def _(d):
+                final_copy(c, d).start()
 
     barrier = pltpu.get_barrier_semaphore()
-    for d in range(1, n_chan):
-        pl.semaphore_signal(barrier, inc=1, device_id={"chan": (me_c + d) % n_chan},
-                            device_id_type=pl.DeviceIdType.MESH)
-    for d in range(1, n_section):
-        pl.semaphore_signal(barrier, inc=1, device_id={"section": (me_s + d) % n_section},
+
+    @pl.loop(1, n_dev)
+    def _(d):
+        to = (me + d) % n_dev
+        pl.semaphore_signal(barrier, inc=1,
+                            device_id={"section": to // n_chan, "chan": to % n_chan},
                             device_id_type=pl.DeviceIdType.MESH)
 
     @pl.loop(0, chunks)
@@ -582,9 +676,9 @@
             power = power_ref[c * kc + k].astype(F32)
             y_ref[c, k, 0] = jnp.where(power > 0, 1.0, 0.0).astype(BF16)
             y_ref[c, k, 1] = jnp.zeros((feeds, LANES), BF16)
-        norm[c, 0] = jnp.zeros((8, LANES), F32)
-
-    pl.semaphore_wait(barrier, n_chan + n_section - 2)
+        norm[c, 0] = jnp.zeros((kc, LANES), F32)
+
+    pl.semaphore_wait(barrier, n_dev - 1)
 
     stages = [(7, add_sections), (3, add_pieces), (5, expand), (4, share_half), (1, add_half),
               (0, project)]
@@ -603,12 +697,7 @@
 
     @pl.loop(0, chunks)
     def _(c):
-        for copy in y_copies(c):
-            copy.wait_send()
-        for copy in y_copies(c, receive=True):
-            copy.wait_recv()
-
-    out_ref[...] = y_ref[...]
+        final_wait(c)
 
 
 def solve(spectra, power, n_section, n_chan):
@@ -619,6 +708,7 @@
     half_rows = kc * blocks
     piece_rows = half_rows // n_z
     k_piece = kc // n_section
+    n_dev = n_section * n_chan
     dma = pltpu.SemaphoreType.DMA
     per = lambda n: dma((chunks, n))
     scratch = [
@@ -627,10 +717,11 @@
         pltpu.VMEM((chunks, 2, half_rows, LANES), F32),
         pltpu.VMEM((chunks, half_rows, LANES), F32),
         pltpu.VMEM((chunks, half_rows, LANES), F32),
-        pltpu.VMEM((chunks, n_z - 1, piece_rows, LANES), F32),
+        pltpu.VMEM((chunks, half_rows, LANES), BF16),
+        pltpu.VMEM((chunks, n_z - 1, piece_rows, LANES), BF16),
         pltpu.VMEM((chunks, 2, half_rows, LANES), F32),
-        pltpu.VMEM((2 * blocks + 8, LANES), F32),
-        pltpu.VMEM((chunks, n_chan, 8, LANES), F32),
+        pltpu.VMEM((3 * blocks + 8, LANES), F32),
+        pltpu.VMEM((chunks, n_chan, kc, LANES), F32),
         pltpu.VMEM((chunks, kc, 2, feeds, LANES), BF16),
         pltpu.VMEM((chunks, n_section - 1, k_piece, 2, feeds, LANES), BF16),
         pltpu.VMEM((chunks, kc, 2, feeds, LANES), BF16),
@@ -640,13 +731,17 @@
         dma((chunks,)), dma((chunks,)),
         per(n_chan - 1), per(n_chan - 1),
         per(n_section - 1), per(n_section - 1), per(n_section - 1), per(n_section - 1),
+        pltpu.VMEM((chunks, n_dev, k_piece, LANES // n_dev, 2 * feeds), F32),
+        dma((chunks,)), dma((chunks,)), dma((chunks,)),
     ]
     vmem = pl.BlockSpec(memory_space=pltpu.VMEM)
     return pl.pallas_call(
         functools.partial(solve_kernel, (n_section, n_chan, feeds, blocks, chunks, kc)),
         in_specs=[pl.BlockSpec(memory_space=pl.ANY), vmem],
-        out_specs=vmem,
-        out_shape=jax.ShapeDtypeStruct((chunks, kc, 2, feeds, LANES), BF16),
+        out_specs=pl.BlockSpec(memory_space=pl.ANY),
+        out_shape=jax.ShapeDtypeStruct(
+            (chunks, n_dev, k_piece, LANES // n_dev, 2 * feeds), F32
+        ),
         scratch_shapes=scratch,
         compiler_params=pltpu.CompilerParams(
             collective_id=1, has_side_effects=True, vmem_limit_bytes=VMEM_LIMIT
@@ -657,19 +752,19 @@
 def local(voltages, usable, auto_power):
     n_section, n_chan = lax.axis_size("section"), lax.axis_size("chan")
     power = (usable.astype(F32) * auto_power).astype(BF16)
-    power = lax.all_to_all(power, "chan", split_axis=1, concat_axis=0, tiled=True)
-    power = lax.all_gather(power, "section", axis=0, tiled=True)
-    feeds_here = power.shape[1]
+    here = power.shape[0]
+    feeds_here = power.shape[1] // n_chan
+    pack = LANES // feeds_here
+    power = power.reshape(pack, here // pack, n_chan, feeds_here).transpose(2, 1, 0, 3)
+    power = power.reshape(n_chan, here // pack, LANES)
+
+    spectra, power = channelize(voltages, power, n_section, n_chan)
+    power = power.reshape(-1, here // pack, pack, feeds_here).transpose(0, 2, 1, 3)
     power = power.reshape(LANES, OUTER, feeds_here).transpose(1, 2, 0)
-
-    spectra = channelize(voltages, n_section)
     result = solve(spectra, power, n_section, n_chan)
-    result = result.reshape(OUTER, 2, feeds_here, LANES)
-    width = LANES // n_section
-    result = lax.dynamic_slice_in_dim(result, lax.axis_index("section") * width, width, axis=3)
-    result = result.transpose(1, 3, 0, 2).reshape(2, width * OUTER, feeds_here)
-    result = lax.all_to_all(result, "chan", split_axis=1, concat_axis=2, tiled=True)
-    result = result.astype(F32)
+    chunks, k_piece = result.shape[0], result.shape[2]
+    result = result.reshape(chunks, n_section, n_chan, k_piece, -1, 2, feeds_here)
+    result = result.transpose(5, 4, 0, 1, 3, 2, 6).reshape(2, here, n_chan * feeds_here)
     length = jnp.sqrt(jnp.sum(result * result, axis=(0, 2)) + epsilon)
     return result / jnp.sqrt(length)[None, :, None]
 

time: 302 us -> 274 us (0.907)
  blocking collectives: 22.3 us -> 0 us
  starting transfers between devices: 6.35 us -> 0 us
    all_to_all x1 -> x0, blocking collectives: 13.3 us -> none  [local(): lax.all_to_all(result, 'chan', split_axis=1, concat_axis=2, tiled=True)]
    all_gather x1 -> x0, blocking collectives: 9.03 us -> none  [local(): power = lax.all_gather(power, 'section', axis=0, tiled=True)]
    all_to_all x1 -> x0, starting transfers between devices: 6.35 us -> none  [local(): lax.all_to_all(power, 'chan', split_axis=1, concat_axis=0, tiled=True)]
    reshape x1 -> x7, local copies, waits for them, and re-layouts: 0.54 us -> 5.97 us  [the longest x2 2.71 us: local(): power.reshape(-1, here // pack, pack, feeds_here).transpose(0, 2, 1, 3)]
    unnamed x6 -> x0, local copies, waits for them, and re-layouts: 3.86 us -> none
    pallas_call x1, Pallas kernels: 92.4 us -> 95.8 us  [channelize(): pl.pallas_call(functools.partial(channelize_kernel, (frames, tiles, early...]
    pallas_call x1, Pallas kernels: 170 us -> 167 us  [solve(): pl.pallas_call(functools.partial(solve_kernel, (n_section, n_chan, feeds,...]
  transfers between devices with their start and end apart: 1 -> 0, of which waited for: 0 -> 0; matrix products, arithmetic and copies ran while one was open for 0% -> 0% of each run, Pallas kernels for 31% -> 0%
where the time goes in v3:
time: 274 us
  Pallas kernels  263 us (96%)
  local copies, waits for them, and re-layouts  8.37 us (3%)
  other arithmetic  2.78 us (1%)
    pallas_call x1, Pallas kernels, solve(): pl.pallas_call(functools.partial(solve_kernel, (n_section, n_chan, feeds,...  167 us
    pallas_call x1, Pallas kernels, channelize(): pl.pallas_call(functools.partial(channelize_kernel, (frames, tiles, early...  95.8 us

profile of v3, /device:TPU:0, one launch (start us, length us, event | category | flops | bytes accessed | tf_op | source)
XLA Modules:
  0.0 273.8 jit_solution(12558152642878870957)
XLA Ops:
  0.0 1.1 multiply_convert_fusion
  1.1 0.2 reshape.31
  1.3 0.3 copy.24
  1.5 0.8 reshape.32.refs_5_
  2.4 95.8 %shard_map.55 = (bf16[32,2,4,32,16,128]{5,4,3,2,1,0:T(8,128)(2,1)}, bf16[32,64,128]{2,1,0:T(8,128)(2,1)}) custom-call(bf16[2,64,131072]{2,1,0:T(8,128)(2,1)} %refs_4_.1, bf16[2,64,131072]{2,1,0:T(8,128)(2,1)} %refs_4_.1, f32[4,32,128]{2,1,0:T(8,128)} %constant.8.clone.refs_2_, f32[4,128,128]{2,1,0:T(8,128)} %constant.9.clone.refs_3_, ...), custom_call_target="tpu_custom_call" | custom-call | tf_op jit(solution)/shard_map/pallas_call | solution.py:306
  98.2 2.5 reshape.33
  100.7 0.3 copy.18
  100.9 1.9 copy.19
  102.8 166.7 %shard_map.56 = f32[8,32,1,4,128]{4,3,2,1,0:T(4,128)} custom-call(bf16[32,2,4,32,16,128]{5,4,3,2,1,0:T(8,128)(2,1)} %get-tuple-element.7.refs_0_, bf16[32,64,128]{2,1,0:T(8,128)(2,1)} %bitcast.15), custom_call_target="tpu_custom_call" | custom-call | tf_op jit(solution)/shard_map/pallas_call | solution.py:738
  269.5 1.7 reshape.35
  271.3 0.8 multiply_reduce_fusion
  272.1 0.1 copy.21
  272.2 0.1 copy.22
  272.3 0.1 sqrt.20
  272.4 0.2 copy.20
  272.6 0.3 reshape.36
  272.9 0.9 broadcast_divide_fusion
  (1 shorter events, 0.0 us)

commit v4 on v3

--- a/solution.py
+++ b/solution.py
@@ -65,8 +65,16 @@
     if n == 1:
         return values
     even, odd = dft(values[0::2]), dft(values[1::2])
-    odd = [times(z, np.exp(-2j * np.pi * k / n)) for k, z in enumerate(odd)]
-    return [plus(a, b) for a, b in zip(even, odd)] + [minus(a, b) for a, b in zip(even, odd)]
+    sums, differences = [], []
+    for k, (a, z) in enumerate(zip(even, odd)):
+        if 4 * k == n:
+            sums.append((a[0] + z[1], a[1] - z[0]))
+            differences.append((a[0] - z[1], a[1] + z[0]))
+        else:
+            z = times(z, np.exp(-2j * np.pi * k / n))
+            sums.append(plus(a, z))
+            differences.append(minus(a, z))
+    return sums + differences
 
 
 QUICK = 8
@@ -242,7 +250,8 @@
             lo = jnp.concatenate([lo_ref[i, 0], lo_ref[i, 1]], axis=1)
             th, tl = high[k1], low[k1]
             dot = functools.partial(jnp.dot, preferred_element_type=F32)
-            res = (dot(hi, th) + dot(lo, th)) + dot(hi, tl)
+            both = dot(jnp.concatenate([hi, lo], axis=0), th)
+            res = (both[:rows] + both[rows:]) + dot(hi, tl)
             for part in range(2):
                 piece = res[:, part * LANES : (part + 1) * LANES].astype(BF16)
                 out_ref[k1, part, 0] = piece.reshape(frames, TILE, LANES)

time: 274 us -> 271 us (0.989)
  Pallas kernels: 263 us -> 259 us
    pallas_call x1, Pallas kernels: 95.8 us -> 92.6 us  [channelize(): pl.pallas_call(functools.partial(channelize_kernel, (frames, tiles, early...]
where the time goes in v4:
time: 271 us
  Pallas kernels  259 us (96%)
  local copies, waits for them, and re-layouts  8.37 us (3%)
  other arithmetic  2.78 us (1%)
    pallas_call x1, Pallas kernels, solve(): pl.pallas_call(functools.partial(solve_kernel, (n_section, n_chan, feeds,...  167 us
    pallas_call x1, Pallas kernels, channelize(): pl.pallas_call(functools.partial(channelize_kernel, (frames, tiles, early...  92.6 us

profile of v4, /device:TPU:0, one launch (start us, length us, event | category | flops | bytes accessed | tf_op | source)
XLA Modules:
  0.0 270.6 jit_solution(6331258450535908892)
XLA Ops:
  0.0 1.1 multiply_convert_fusion
  1.1 0.2 reshape.31
  1.3 0.3 copy.24
  1.5 0.8 reshape.32.refs_5_
  2.4 92.6 %shard_map.55 = (bf16[32,2,4,32,16,128]{5,4,3,2,1,0:T(8,128)(2,1)}, bf16[32,64,128]{2,1,0:T(8,128)(2,1)}) custom-call(bf16[2,64,131072]{2,1,0:T(8,128)(2,1)} %refs_4_.1, bf16[2,64,131072]{2,1,0:T(8,128)(2,1)} %refs_4_.1, f32[4,32,128]{2,1,0:T(8,128)} %constant.8.clone.refs_2_, f32[4,128,128]{2,1,0:T(8,128)} %constant.9.clone.refs_3_, ...), custom_call_target="tpu_custom_call" | custom-call | tf_op jit(solution)/shard_map/pallas_call | solution.py:315
  95.0 2.5 reshape.33
  97.4 0.3 copy.18
  97.7 1.9 copy.19
  99.6 166.8 %shard_map.56 = f32[8,32,1,4,128]{4,3,2,1,0:T(4,128)} custom-call(bf16[32,2,4,32,16,128]{5,4,3,2,1,0:T(8,128)(2,1)} %get-tuple-element.7.refs_0_, bf16[32,64,128]{2,1,0:T(8,128)(2,1)} %bitcast.15), custom_call_target="tpu_custom_call" | custom-call | tf_op jit(solution)/shard_map/pallas_call | solution.py:747
  266.4 1.7 reshape.35
  268.1 0.8 multiply_reduce_fusion
  268.9 0.1 copy.21
  269.0 0.1 copy.22
  269.1 0.1 sqrt.20
  269.2 0.2 copy.20
  269.5 0.3 reshape.36
  269.7 0.9 broadcast_divide_fusion
  (1 shorter events, 0.0 us)
